TPU v7x, 256 devices: a whole 4x4x8 slice. The times are simulated.
256 devices in a mesh: row: 8 (over x, y_hi), col: 32 (over z, y_lo, core).
Axes of the slice: x: 4, y: 4 (y_hi: 2, y_lo: 2; y = y_hi * 2 + y_lo), z: 8, core: 2. Of those that a mesh axis runs over, the one named last changes fastest.
Arguments:
- e_field: float32 [3, 64, 64, 4096], P(None, None, 'row', 'col'), may hold values from -6 to 6
- h_field: float32 [3, 64, 64, 4096], P(None, None, 'row', 'col'), may hold values from -6 to 6
- e_coef: float32 [64, 64, 4096], P(None, 'row', 'col'), may hold values from 0.125 to 0.5
- basis: float32 [128, 64, 4096], P('row', None, 'col'), may hold values from -0.01171875 to 0.01171875
- pml_width: int32 [4], replicated, may hold values from 2 to 8
- snap_index: int32 [64], replicated, may hold values from 0 to 383
Outputs:
- e_final: float32 [3, 64, 64, 4096], P(None, None, 'row', 'col')
- h_final: float32 [3, 64, 64, 4096], P(None, None, 'row', 'col')
- coefficients: float32 [64, 128], replicated
- gram: float32 [64, 64], replicated
All inputs are finite; a program needn't handle non-finite values.
Results may differ from a plain program's by a relative error of at most 0.00008.
Values sent between devices are 32-bit elements; how exact they have to be, the bound alone decides.
No kernel may reach another device: no remote copies, remote signals or barrier semaphores. Data moves between devices by JAX's collectives and lax.ppermute only.
A program may use at most 64 MiB of HBM per device.

v0:
```python
import jax
import jax.numpy as jnp
from jax import lax
from jax.sharding import Mesh
from jax.sharding import PartitionSpec as P

STEPS = 8
ROW = ("row_0", "row_1")
COL = ("col_0", "col_1", "col_2")
ROW_COL = ("row_0", "row_1", "col_0", "col_1", "col_2")


time_step = 0.5
sigma_top = 4.0
alpha_shift = 0.05


def from_behind(block, axis, distance):
    devices = range(lax.axis_size(axis))
    route = [(i - distance, i) for i in devices if i - distance in devices]
    return lax.ppermute(block, axis, route)


def by_axis(array, axes):
    for axis in axes:
        array = lax.psum(array, axis)
    return array


def forward(field, axis, plane):
    count = field.shape[axis]
    after = jnp.concatenate(
        [lax.slice_in_dim(field, 1, count, axis=axis), jnp.expand_dims(plane, axis)], axis
    )
    return after - field


def backward(field, axis, plane):
    count = field.shape[axis]
    before = jnp.concatenate(
        [jnp.expand_dims(plane, axis), lax.slice_in_dim(field, 0, count - 1, axis=axis)], axis
    )
    return field - before


def absorber(positions, total, low, high):
    depth = jnp.maximum(
        jnp.maximum((low - positions) / low, (positions - (total - 1.0 - high)) / high), 0.0
    )
    sigma = sigma_top * depth**3
    damp = jnp.exp(-(sigma + alpha_shift) * time_step)
    gain = sigma / (sigma + alpha_shift) * (damp - 1.0)
    return (damp, gain)


def magnetic(e_field, h_field, psi, next_x, next_y, damp_x, gain_x, damp_y, gain_y):
    e_x, e_y, e_z = (e_field[0], e_field[1], e_field[2])
    h_x, h_y, h_z = (h_field[0], h_field[1], h_field[2])
    zplane = jnp.zeros_like(e_x[0])
    ez_dy = forward(e_z, 2, next_y[1])
    ey_dz = forward(e_y, 0, zplane)
    ex_dz = forward(e_x, 0, zplane)
    ez_dx = forward(e_z, 1, next_x[1])
    ey_dx = forward(e_y, 1, next_x[0])
    ex_dy = forward(e_x, 2, next_y[0])
    psi_hxy = damp_y * psi[0] + gain_y * ez_dy
    psi_hyx = damp_x * psi[1] + gain_x * ez_dx
    psi_hzx = damp_x * psi[2] + gain_x * ey_dx
    psi_hzy = damp_y * psi[3] + gain_y * ex_dy
    h_x = h_x - time_step * (ez_dy + psi_hxy - ey_dz)
    h_y = h_y - time_step * (ex_dz - ez_dx - psi_hyx)
    h_z = h_z - time_step * (ey_dx + psi_hzx - ex_dy - psi_hzy)
    return (jnp.stack((h_x, h_y, h_z)), (psi_hxy, psi_hyx, psi_hzx, psi_hzy))


def electric(e_field, h_field, psi, e_coef, prev_x, prev_y, damp_x, gain_x, damp_y, gain_y):
    e_x, e_y, e_z = (e_field[0], e_field[1], e_field[2])
    h_x, h_y, h_z = (h_field[0], h_field[1], h_field[2])
    zplane = jnp.zeros_like(h_x[0])
    hz_dy = backward(h_z, 2, prev_y[1])
    hy_dz = backward(h_y, 0, zplane)
    hx_dz = backward(h_x, 0, zplane)
    hz_dx = backward(h_z, 1, prev_x[1])
    hy_dx = backward(h_y, 1, prev_x[0])
    hx_dy = backward(h_x, 2, prev_y[0])
    psi_exy = damp_y * psi[0] + gain_y * hz_dy
    psi_eyx = damp_x * psi[1] + gain_x * hz_dx
    psi_ezx = damp_x * psi[2] + gain_x * hy_dx
    psi_ezy = damp_y * psi[3] + gain_y * hx_dy
    e_x = e_x + e_coef * (hz_dy + psi_exy - hy_dz)
    e_y = e_y + e_coef * (hx_dz - hz_dx - psi_eyx)
    e_z = e_z + e_coef * (hy_dx + psi_ezx - hx_dy - psi_ezy)
    return (jnp.stack((e_x, e_y, e_z)), (psi_exy, psi_eyx, psi_ezx, psi_ezy))


def shards(e_field, h_field, e_coef, basis, pml_width, snap_index):
    depth_z, rows_here, cols_here = e_coef.shape
    full_x = rows_here * lax.axis_size(ROW)
    full_y = cols_here * lax.axis_size(COL)
    x_first = lax.axis_index(ROW) * rows_here
    y_first = lax.axis_index(COL) * cols_here
    widths = pml_width.astype(jnp.float32)
    x_pos = x_first.astype(jnp.float32) + jnp.arange(rows_here, dtype=jnp.float32)
    y_pos = y_first.astype(jnp.float32) + jnp.arange(cols_here, dtype=jnp.float32)
    hdx, hgx = absorber(x_pos + 0.5, float(full_x), widths[0], widths[1])
    hdy, hgy = absorber(y_pos + 0.5, float(full_y), widths[2], widths[3])
    edx, egx = absorber(x_pos, float(full_x), widths[0], widths[1])
    edy, egy = absorber(y_pos, float(full_y), widths[2], widths[3])
    hdx, hgx, edx, egx = [v.reshape(1, rows_here, 1) for v in (hdx, hgx, edx, egx)]
    hdy, hgy, edy, egy = [v.reshape(1, 1, cols_here) for v in (hdy, hgy, edy, egy)]
    zeros_cells = jnp.zeros((depth_z, rows_here, cols_here), jnp.float32)
    psi_mag = (zeros_cells,) * 4
    psi_ele = (zeros_cells,) * 4
    for step in range(STEPS):
        next_x = from_behind(e_field[1:3, :, 0, :], ROW, -1)
        next_y = from_behind(jnp.stack((e_field[0, :, :, 0], e_field[2, :, :, 0])), COL, -1)
        h_field, psi_mag = magnetic(e_field, h_field, psi_mag, next_x, next_y, hdx, hgx, hdy, hgy)
        prev_x = from_behind(h_field[1:3, :, -1, :], ROW, 1)
        prev_y = from_behind(jnp.stack((h_field[0, :, :, -1], h_field[2, :, :, -1])), COL, 1)
        e_field, psi_ele = electric(
            e_field, h_field, psi_ele, e_coef, prev_x, prev_y, edx, egx, edy, egy
        )
    planes = jnp.concatenate((e_field, h_field), 0).reshape(6 * depth_z, rows_here, cols_here)
    snaps = jnp.take(planes, snap_index, axis=0)
    count = snaps.shape[0]
    flat = snaps.reshape(count, rows_here * cols_here)
    gram_part = jnp.dot(flat, flat.T, precision=lax.Precision.HIGHEST) / float(full_x * full_y)
    local_modes = lax.all_to_all(basis, ROW, split_axis=1, concat_axis=0, tiled=True)
    coef_part = jnp.dot(
        flat, local_modes.reshape(local_modes.shape[0], -1).T, precision=lax.Precision.HIGHEST
    )
    coefficients, gram = (by_axis(coef_part, ROW_COL), by_axis(gram_part, ROW_COL))
    return (e_field, h_field, coefficients, gram)


def solution(mesh):
    split = Mesh(mesh.devices.reshape(4, 2, 8, 2, 2), ("row_0", "row_1", "col_0", "col_1", "col_2"))
    return jax.shard_map(
        shards,
        mesh=split,
        in_specs=(
            P(None, None, ROW, COL),
            P(None, None, ROW, COL),
            P(None, ROW, COL),
            P(ROW, None, COL),
            P(),
            P(),
        ),
        out_specs=(P(None, None, ROW, COL), P(None, None, ROW, COL), P(), P()),
        check_vma=False,
    )
```

profile of v0, /device:TPU:1, one launch (start us, length us, event | category | flops | bytes accessed | tf_op | source)
XLA Modules:
  0.0 416.5 jit_solution(7778291619104819544)
XLA Ops:
  4.5 5.1 %collective-permute-start.1 = (f32[2,64,8]{1,2,0:T(8,128)S(1)}, f32[2,64,8]{1,2,0:T(8,128)S(1)}, u32[]{:S(2)}, u32[]{:S(2)}) collective-permute-start(f32[2,64,8]{1,2,0:T(8,128)S(1)} %pad_maximum_fusion.17), channel_id=1, source_target_pairs={{1,0},{2,1},{3,2},{4,3},{5,4},{6,5},{7,6},{8,7},{9,8},{10,9},{11,1... | collective-permute-start | bytes 12296 | tf_op jit(solution)/shard_map/ppermute | solution.py:21
  10.7 6.4 %all-to-all-start = ((f32[16,64,128]{2,0,1:T(8,128)}), f32[16,64,128]{2,0,1:T(8,128)}, u32[]{:S(2)}, u32[]{:S(2)}) async-start(f32[16,64,128]{2,0,1:T(8,128)} %copy.1592), calls=%async_computation | async-start | bytes 1048576 | tf_op jit(solution)/shard_map/all_to_all | solution.py:128
  31.1 2.2 bitcast_subtract_fusion.1
  33.6 3.4 collective-permute-start.2
  39.9 5.7 %collective-permute-start.3 = (f32[2,64,128]{2,1,0:T(8,128)S(1)}, f32[2,64,128]{2,1,0:T(8,128)S(1)}, u32[]{:S(2)}, u32[]{:S(2)}) collective-permute-start(f32[2,64,128]{2,1,0:T(8,128)S(1)} %bitcast.519), channel_id=1, source_target_pairs={{0,32},{32,64},{64,96},{96,128},{128,160},{160,192},{192,224},{1,3... | collective-permute-start | bytes 196616 | tf_op jit(solution)/shard_map/ppermute | solution.py:21
  59.0 3.7 collective-permute-done.4
  62.6 2.3 multiply_subtract_fusion.20
  65.2 2.4 multiply_subtract_fusion.19
  67.9 4.8 %collective-permute-start.6 = (f32[2,64,8]{1,2,0:T(8,128)S(1)}, f32[2,64,8]{1,2,0:T(8,128)S(1)}, u32[]{:S(2)}, u32[]{:S(2)}) collective-permute-start(f32[2,64,8]{1,2,0:T(8,128)S(1)} %pad_maximum_fusion.20), channel_id=1, source_target_pairs={{0,1},{1,2},{2,3},{3,4},{4,5},{5,6},{6,7},{7,8},{8,9},{9,10},{10,1... | collective-permute-start | bytes 12296 | tf_op jit(solution)/shard_map/ppermute | solution.py:21
  74.1 5.9 %collective-permute-start.7 = (f32[2,64,128]{2,1,0:T(8,128)}, f32[2,64,128]{2,1,0:T(8,128)}, u32[]{:S(2)}, u32[]{:S(2)}) collective-permute-start(f32[2,64,128]{2,1,0:T(8,128)} %fusion.15), channel_id=1, source_target_pairs={{0,32},{32,64},{64,96},{96,128},{128,160},{160,192},{192,224},{1,3... | collective-permute-start | bytes 196616 | tf_op jit(solution)/shard_map/ppermute | solution.py:21
  101.2 2.3 multiply_subtract_fusion.17
  104.5 5.1 %collective-permute-start.10 = (f32[2,64,8]{1,2,0:T(8,128)S(1)}, f32[2,64,8]{1,2,0:T(8,128)S(1)}, u32[]{:S(2)}, u32[]{:S(2)}) collective-permute-start(f32[2,64,8]{1,2,0:T(8,128)S(1)} %pad_maximum_fusion.22), channel_id=1, source_target_pairs={{0,1},{1,2},{2,3},{3,4},{4,5},{5,6},{6,7},{7,8},{8,9},{9,10},{10,1... | collective-permute-start | bytes 12296 | tf_op jit(solution)/shard_map/ppermute | solution.py:21
  113.2 4.9 %collective-permute-start.11 = (f32[2,64,128]{2,1,0:T(8,128)}, f32[2,64,128]{2,1,0:T(8,128)}, u32[]{:S(2)}, u32[]{:S(2)}) collective-permute-start(f32[2,64,128]{2,1,0:T(8,128)} %bitcast.74), channel_id=1, source_target_pairs={{0,32},{32,64},{64,96},{96,128},{128,160},{160,192},{192,224},{1,3... | collective-permute-start | bytes 196616 | tf_op jit(solution)/shard_map/ppermute | solution.py:21
  136.6 2.3 multiply_subtract_fusion.13
  142.2 2.3 multiply_subtract_fusion.14
  145.5 5.0 %collective-permute-start.14 = (f32[2,64,8]{1,2,0:T(8,128)S(1)}, f32[2,64,8]{1,2,0:T(8,128)S(1)}, u32[]{:S(2)}, u32[]{:S(2)}) collective-permute-start(f32[2,64,8]{1,2,0:T(8,128)S(1)} %pad_maximum_fusion.24), channel_id=1, source_target_pairs={{0,1},{1,2},{2,3},{3,4},{4,5},{5,6},{6,7},{7,8},{8,9},{9,10},{10,1... | collective-permute-start | bytes 12296 | tf_op jit(solution)/shard_map/ppermute | solution.py:21
  153.2 5.6 %collective-permute-start.15 = (f32[2,64,128]{2,1,0:T(8,128)}, f32[2,64,128]{2,1,0:T(8,128)}, u32[]{:S(2)}, u32[]{:S(2)}) collective-permute-start(f32[2,64,128]{2,1,0:T(8,128)} %fusion.12), channel_id=1, source_target_pairs={{0,32},{32,64},{64,96},{96,128},{128,160},{160,192},{192,224},{1,3... | collective-permute-start | bytes 196616 | tf_op jit(solution)/shard_map/ppermute | solution.py:21
  181.6 2.4 multiply_subtract_fusion.11
  185.0 5.2 %collective-permute-start.18 = (f32[2,64,8]{1,2,0:T(8,128)S(1)}, f32[2,64,8]{1,2,0:T(8,128)S(1)}, u32[]{:S(2)}, u32[]{:S(2)}) collective-permute-start(f32[2,64,8]{1,2,0:T(8,128)S(1)} %pad_maximum_fusion.26), channel_id=1, source_target_pairs={{0,1},{1,2},{2,3},{3,4},{4,5},{5,6},{6,7},{7,8},{8,9},{9,10},{10,1... | collective-permute-start | bytes 12296 | tf_op jit(solution)/shard_map/ppermute | solution.py:21
  193.2 4.4 %collective-permute-start.19 = (f32[2,64,128]{2,1,0:T(8,128)S(1)}, f32[2,64,128]{2,1,0:T(8,128)}, u32[]{:S(2)}, u32[]{:S(2)}) collective-permute-start(f32[2,64,128]{2,1,0:T(8,128)S(1)} %bitcast.521), channel_id=1, source_target_pairs={{0,32},{32,64},{64,96},{96,128},{128,160},{160,192},{192,224},{1,3... | collective-permute-start | bytes 196616 | tf_op jit(solution)/shard_map/ppermute | solution.py:21
  223.1 2.3 multiply_subtract_fusion.8
  227.2 4.8 %collective-permute-start.22 = (f32[2,64,8]{1,2,0:T(8,128)S(1)}, f32[2,64,8]{1,2,0:T(8,128)S(1)}, u32[]{:S(2)}, u32[]{:S(2)}) collective-permute-start(f32[2,64,8]{1,2,0:T(8,128)S(1)} %pad_maximum_fusion.28), channel_id=1, source_target_pairs={{0,1},{1,2},{2,3},{3,4},{4,5},{5,6},{6,7},{7,8},{8,9},{9,10},{10,1... | collective-permute-start | bytes 12296 | tf_op jit(solution)/shard_map/ppermute | solution.py:21
  234.6 5.8 %collective-permute-start.23 = (f32[2,64,128]{2,1,0:T(8,128)}, f32[2,64,128]{2,1,0:T(8,128)}, u32[]{:S(2)}, u32[]{:S(2)}) collective-permute-start(f32[2,64,128]{2,1,0:T(8,128)} %fusion.9), channel_id=1, source_target_pairs={{0,32},{32,64},{64,96},{96,128},{128,160},{160,192},{192,224},{1,3... | collective-permute-start | bytes 196616 | tf_op jit(solution)/shard_map/ppermute | solution.py:21
  266.7 5.9 %collective-permute-start.26 = (f32[2,64,8]{1,2,0:T(8,128)S(1)}, f32[2,64,8]{1,2,0:T(8,128)S(1)}, u32[]{:S(2)}, u32[]{:S(2)}) collective-permute-start(f32[2,64,8]{1,2,0:T(8,128)S(1)} %pad_maximum_fusion.30), channel_id=1, source_target_pairs={{0,1},{1,2},{2,3},{3,4},{4,5},{5,6},{6,7},{7,8},{8,9},{9,10},{10,1... | collective-permute-start | bytes 12296 | tf_op jit(solution)/shard_map/ppermute | solution.py:21
  276.1 5.5 %collective-permute-start.27 = (f32[2,64,128]{2,1,0:T(8,128)}, f32[2,64,128]{2,1,0:T(8,128)}, u32[]{:S(2)}, u32[]{:S(2)}) collective-permute-start(f32[2,64,128]{2,1,0:T(8,128)} %fusion.8), channel_id=1, source_target_pairs={{0,32},{32,64},{64,96},{96,128},{128,160},{160,192},{192,224},{1,3... | collective-permute-start | bytes 196616 | tf_op jit(solution)/shard_map/ppermute | solution.py:21
  308.6 4.8 %collective-permute-start.30 = (f32[2,64,8]{1,2,0:T(8,128)S(1)}, f32[2,64,8]{1,2,0:T(8,128)S(1)}, u32[]{:S(2)}, u32[]{:S(2)}) collective-permute-start(f32[2,64,8]{1,2,0:T(8,128)S(1)} %pad_maximum_fusion.32), channel_id=1, source_target_pairs={{0,1},{1,2},{2,3},{3,4},{4,5},{5,6},{6,7},{7,8},{8,9},{9,10},{10,1... | collective-permute-start | bytes 12296 | tf_op jit(solution)/shard_map/ppermute | solution.py:21
  316.5 6.5 %collective-permute-start.31 = (f32[2,64,128]{2,1,0:T(8,128)S(1)}, f32[2,64,128]{2,1,0:T(8,128)}, u32[]{:S(2)}, u32[]{:S(2)}) collective-permute-start(f32[2,64,128]{2,1,0:T(8,128)S(1)} %bitcast.520), channel_id=1, source_target_pairs={{0,32},{32,64},{64,96},{96,128},{128,160},{160,192},{192,224},{1,3... | collective-permute-start | bytes 196616 | tf_op jit(solution)/shard_map/ppermute | solution.py:21
  334.9 13.8 %all-reduce.33 = (f32[64,128]{1,0:T(8,128)S(1)}, f32[64,64]{1,0:T(8,128)S(1)}) all-reduce(f32[64,128]{1,0:T(8,128)S(1)} %fusion.1, f32[64,64]{1,0:T(8,128)S(1)} %fusion), channel_id=1, replica_groups=mesh['row_0'=4,'row_1'=2,'col_0'=8,'col_1'=2,'col_2'=2] {'row_0'}, use_global_device_ids=true, to_apply=%region_0.1 | all-reduce | flops 12288 | bytes 98304 | tf_op jit(solution)/shard_map/psum | solution.py:26
  348.7 7.6 %all-reduce.36 = (f32[64,128]{1,0:T(8,128)S(1)}, f32[64,64]{1,0:T(8,128)S(1)}) all-reduce(f32[64,128]{1,0:T(8,128)S(1)} %get-tuple-element.18, f32[64,64]{1,0:T(8,128)S(1)} %get-tuple-element.19), channel_id=1, replica_groups=mesh['row_0'=4,'row_1'=2,'col_0'=8,'col_1'=2,'col_2'=2] {'row_1'}, use_global_device_ids=true, to_apply=%region_1.2 | all-reduce | flops 12288 | bytes 98304 | tf_op jit(solution)/shard_map/psum | solution.py:26
  356.3 30.5 %all-reduce.32 = (f32[64,128]{1,0:T(8,128)S(1)}, f32[64,64]{1,0:T(8,128)S(1)}) all-reduce(f32[64,128]{1,0:T(8,128)S(1)} %get-tuple-element.24, f32[64,64]{1,0:T(8,128)S(1)} %get-tuple-element.25), channel_id=1, replica_groups=mesh['row_0'=4,'row_1'=2,'col_0'=8,'col_1'=2,'col_2'=2] {'col_0'}, use_global_device_ids=true, to_apply=%region_2.3 | all-reduce | flops 12288 | bytes 98304 | tf_op jit(solution)/shard_map/psum | solution.py:26
  386.8 13.4 %all-reduce.35 = (f32[64,128]{1,0:T(8,128)S(1)}, f32[64,64]{1,0:T(8,128)S(1)}) all-reduce(f32[64,128]{1,0:T(8,128)S(1)} %get-tuple-element.16, f32[64,64]{1,0:T(8,128)S(1)} %get-tuple-element.17), channel_id=1, replica_groups=mesh['row_0'=4,'row_1'=2,'col_0'=8,'col_1'=2,'col_2'=2] {'col_1'}, use_global_device_ids=true, to_apply=%region_3.4 | all-reduce | flops 12288 | bytes 98304 | tf_op jit(solution)/shard_map/psum | solution.py:26
  400.1 15.4 %all-reduce.34 = (f32[64,128]{1,0:T(8,128)}, f32[64,64]{1,0:T(8,128)}) all-reduce(f32[64,128]{1,0:T(8,128)S(1)} %get-tuple-element.22, f32[64,64]{1,0:T(8,128)S(1)} %get-tuple-element.23), channel_id=1, replica_groups=mesh['row_0'=4,'row_1'=2,'col_0'=8,'col_1'=2,'col_2'=2] {'col_2'}, use_global_device_ids=true, to_apply=%region_4.5 | all-reduce | flops 12288 | bytes 98304 | tf_op jit(solution)/shard_map/psum | solution.py:26
  (559 shorter events, 214.7 us)
Async XLA Ops:
  1.8 26.5 %collective-permute-start = (f32[2,64,128]{2,1,0:T(8,128)S(1)}, f32[2,64,128]{2,1,0:T(8,128)}, u32[]{:S(2)}, u32[]{:S(2)}) collective-permute-start(f32[2,64,128]{2,1,0:T(8,128)S(1)} %bitcast.522), channel_id=1, source_target_pairs={{32,0},{64,32},{96,64},{128,96},{160,128},{192,160},{224,192},{33,... | collective-permute-start | bytes 196616 | tf_op jit(solution)/shard_map/ppermute | solution.py:21
  4.5 22.6 %collective-permute-start.1 = (f32[2,64,8]{1,2,0:T(8,128)S(1)}, f32[2,64,8]{1,2,0:T(8,128)S(1)}, u32[]{:S(2)}, u32[]{:S(2)}) collective-permute-start(f32[2,64,8]{1,2,0:T(8,128)S(1)} %pad_maximum_fusion.17), channel_id=1, source_target_pairs={{1,0},{2,1},{3,2},{4,3},{5,4},{6,5},{7,6},{8,7},{9,8},{10,9},{11,1... | collective-permute-start | bytes 12296 | tf_op jit(solution)/shard_map/ppermute | solution.py:21
  10.7 148.1 %all-to-all-start = ((f32[16,64,128]{2,0,1:T(8,128)}), f32[16,64,128]{2,0,1:T(8,128)}, u32[]{:S(2)}, u32[]{:S(2)}) async-start(f32[16,64,128]{2,0,1:T(8,128)} %copy.1592), calls=%async_computation | async-start | bytes 1048576 | tf_op jit(solution)/shard_map/all_to_all | solution.py:128
  33.6 12.0 %collective-permute-start.2 = (f32[2,64,8]{1,2,0:T(8,128)S(1)}, f32[2,64,8]{1,2,0:T(8,128)S(1)}, u32[]{:S(2)}, u32[]{:S(2)}) collective-permute-start(f32[2,64,8]{1,2,0:T(8,128)S(1)} %pad_maximum_fusion.18), channel_id=1, source_target_pairs={{0,1},{1,2},{2,3},{3,4},{4,5},{5,6},{6,7},{7,8},{8,9},{9,10},{10,1... | collective-permute-start | bytes 12296 | tf_op jit(solution)/shard_map/ppermute | solution.py:21
  39.9 8.0 %collective-permute-start.3 = (f32[2,64,128]{2,1,0:T(8,128)S(1)}, f32[2,64,128]{2,1,0:T(8,128)S(1)}, u32[]{:S(2)}, u32[]{:S(2)}) collective-permute-start(f32[2,64,128]{2,1,0:T(8,128)S(1)} %bitcast.519), channel_id=1, source_target_pairs={{0,32},{32,64},{64,96},{96,128},{128,160},{160,192},{192,224},{1,3... | collective-permute-start | bytes 196616 | tf_op jit(solution)/shard_map/ppermute | solution.py:21
  50.2 7.0 %collective-permute-start.5 = (f32[2,64,8]{1,2,0:T(8,128)S(1)}, f32[2,64,8]{1,2,0:T(8,128)S(1)}, u32[]{:S(2)}, u32[]{:S(2)}) collective-permute-start(f32[2,64,8]{1,2,0:T(8,128)S(1)} %pad_maximum_fusion.19), channel_id=1, source_target_pairs={{1,0},{2,1},{3,2},{4,3},{5,4},{6,5},{7,6},{8,7},{9,8},{10,9},{11,1... | collective-permute-start | bytes 12296 | tf_op jit(solution)/shard_map/ppermute | solution.py:21
  55.9 6.7 %collective-permute-start.4 = (f32[2,64,128]{2,1,0:T(8,128)}, f32[2,64,128]{2,1,0:T(8,128)S(1)}, u32[]{:S(2)}, u32[]{:S(2)}) collective-permute-start(f32[2,64,128]{2,1,0:T(8,128)} %fusion.16), channel_id=1, source_target_pairs={{32,0},{64,32},{96,64},{128,96},{160,128},{192,160},{224,192},{33,... | collective-permute-start | bytes 196616 | tf_op jit(solution)/shard_map/ppermute | solution.py:21
  67.9 12.2 %collective-permute-start.6 = (f32[2,64,8]{1,2,0:T(8,128)S(1)}, f32[2,64,8]{1,2,0:T(8,128)S(1)}, u32[]{:S(2)}, u32[]{:S(2)}) collective-permute-start(f32[2,64,8]{1,2,0:T(8,128)S(1)} %pad_maximum_fusion.20), channel_id=1, source_target_pairs={{0,1},{1,2},{2,3},{3,4},{4,5},{5,6},{6,7},{7,8},{8,9},{9,10},{10,1... | collective-permute-start | bytes 12296 | tf_op jit(solution)/shard_map/ppermute | solution.py:21
  74.1 10.2 %collective-permute-start.7 = (f32[2,64,128]{2,1,0:T(8,128)}, f32[2,64,128]{2,1,0:T(8,128)}, u32[]{:S(2)}, u32[]{:S(2)}) collective-permute-start(f32[2,64,128]{2,1,0:T(8,128)} %fusion.15), channel_id=1, source_target_pairs={{0,32},{32,64},{64,96},{96,128},{128,160},{160,192},{192,224},{1,3... | collective-permute-start | bytes 196616 | tf_op jit(solution)/shard_map/ppermute | solution.py:21
  88.0 6.9 %collective-permute-start.9 = (f32[2,64,8]{1,2,0:T(8,128)S(1)}, f32[2,64,8]{1,2,0:T(8,128)S(1)}, u32[]{:S(2)}, u32[]{:S(2)}) collective-permute-start(f32[2,64,8]{1,2,0:T(8,128)S(1)} %pad_maximum_fusion.21), channel_id=1, source_target_pairs={{1,0},{2,1},{3,2},{4,3},{5,4},{6,5},{7,6},{8,7},{9,8},{10,9},{11,1... | collective-permute-start | bytes 12296 | tf_op jit(solution)/shard_map/ppermute | solution.py:21
  93.6 6.8 %collective-permute-start.8 = (f32[2,64,128]{2,1,0:T(8,128)}, f32[2,64,128]{2,1,0:T(8,128)}, u32[]{:S(2)}, u32[]{:S(2)}) collective-permute-start(f32[2,64,128]{2,1,0:T(8,128)} %fusion.14), channel_id=1, source_target_pairs={{32,0},{64,32},{96,64},{128,96},{160,128},{192,160},{224,192},{33,... | collective-permute-start | bytes 196616 | tf_op jit(solution)/shard_map/ppermute | solution.py:21
  104.5 13.6 %collective-permute-start.10 = (f32[2,64,8]{1,2,0:T(8,128)S(1)}, f32[2,64,8]{1,2,0:T(8,128)S(1)}, u32[]{:S(2)}, u32[]{:S(2)}) collective-permute-start(f32[2,64,8]{1,2,0:T(8,128)S(1)} %pad_maximum_fusion.22), channel_id=1, source_target_pairs={{0,1},{1,2},{2,3},{3,4},{4,5},{5,6},{6,7},{7,8},{8,9},{9,10},{10,1... | collective-permute-start | bytes 12296 | tf_op jit(solution)/shard_map/ppermute | solution.py:21
  113.2 9.7 %collective-permute-start.11 = (f32[2,64,128]{2,1,0:T(8,128)}, f32[2,64,128]{2,1,0:T(8,128)}, u32[]{:S(2)}, u32[]{:S(2)}) collective-permute-start(f32[2,64,128]{2,1,0:T(8,128)} %bitcast.74), channel_id=1, source_target_pairs={{0,32},{32,64},{64,96},{96,128},{128,160},{160,192},{192,224},{1,3... | collective-permute-start | bytes 196616 | tf_op jit(solution)/shard_map/ppermute | solution.py:21
  127.8 7.9 %collective-permute-start.13 = (f32[2,64,8]{1,2,0:T(8,128)S(1)}, f32[2,64,8]{1,2,0:T(8,128)S(1)}, u32[]{:S(2)}, u32[]{:S(2)}) collective-permute-start(f32[2,64,8]{1,2,0:T(8,128)S(1)} %pad_maximum_fusion.23), channel_id=1, source_target_pairs={{1,0},{2,1},{3,2},{4,3},{5,4},{6,5},{7,6},{8,7},{9,8},{10,9},{11,1... | collective-permute-start | bytes 12296 | tf_op jit(solution)/shard_map/ppermute | solution.py:21
  134.2 7.2 %collective-permute-start.12 = (f32[2,64,128]{2,1,0:T(8,128)}, f32[2,64,128]{2,1,0:T(8,128)}, u32[]{:S(2)}, u32[]{:S(2)}) collective-permute-start(f32[2,64,128]{2,1,0:T(8,128)} %fusion.13), channel_id=1, source_target_pairs={{32,0},{64,32},{96,64},{128,96},{160,128},{192,160},{224,192},{33,... | collective-permute-start | bytes 196616 | tf_op jit(solution)/shard_map/ppermute | solution.py:21
  145.5 15.3 %collective-permute-start.14 = (f32[2,64,8]{1,2,0:T(8,128)S(1)}, f32[2,64,8]{1,2,0:T(8,128)S(1)}, u32[]{:S(2)}, u32[]{:S(2)}) collective-permute-start(f32[2,64,8]{1,2,0:T(8,128)S(1)} %pad_maximum_fusion.24), channel_id=1, source_target_pairs={{0,1},{1,2},{2,3},{3,4},{4,5},{5,6},{6,7},{7,8},{8,9},{9,10},{10,1... | collective-permute-start | bytes 12296 | tf_op jit(solution)/shard_map/ppermute | solution.py:21
  153.2 13.2 %collective-permute-start.15 = (f32[2,64,128]{2,1,0:T(8,128)}, f32[2,64,128]{2,1,0:T(8,128)}, u32[]{:S(2)}, u32[]{:S(2)}) collective-permute-start(f32[2,64,128]{2,1,0:T(8,128)} %fusion.12), channel_id=1, source_target_pairs={{0,32},{32,64},{64,96},{96,128},{128,160},{160,192},{192,224},{1,3... | collective-permute-start | bytes 196616 | tf_op jit(solution)/shard_map/ppermute | solution.py:21
  173.9 6.9 %collective-permute-start.16 = (f32[2,64,128]{2,1,0:T(8,128)}, f32[2,64,128]{2,1,0:T(8,128)}, u32[]{:S(2)}, u32[]{:S(2)}) collective-permute-start(f32[2,64,128]{2,1,0:T(8,128)} %fusion.11), channel_id=1, source_target_pairs={{32,0},{64,32},{96,64},{128,96},{160,128},{192,160},{224,192},{33,... | collective-permute-start | bytes 196616 | tf_op jit(solution)/shard_map/ppermute | solution.py:21
  185.0 12.6 %collective-permute-start.18 = (f32[2,64,8]{1,2,0:T(8,128)S(1)}, f32[2,64,8]{1,2,0:T(8,128)S(1)}, u32[]{:S(2)}, u32[]{:S(2)}) collective-permute-start(f32[2,64,8]{1,2,0:T(8,128)S(1)} %pad_maximum_fusion.26), channel_id=1, source_target_pairs={{0,1},{1,2},{2,3},{3,4},{4,5},{5,6},{6,7},{7,8},{8,9},{9,10},{10,1... | collective-permute-start | bytes 12296 | tf_op jit(solution)/shard_map/ppermute | solution.py:21
  193.2 10.3 %collective-permute-start.19 = (f32[2,64,128]{2,1,0:T(8,128)S(1)}, f32[2,64,128]{2,1,0:T(8,128)}, u32[]{:S(2)}, u32[]{:S(2)}) collective-permute-start(f32[2,64,128]{2,1,0:T(8,128)S(1)} %bitcast.521), channel_id=1, source_target_pairs={{0,32},{32,64},{64,96},{96,128},{128,160},{160,192},{192,224},{1,3... | collective-permute-start | bytes 196616 | tf_op jit(solution)/shard_map/ppermute | solution.py:21
  209.1 7.7 %collective-permute-start.21 = (f32[2,64,8]{1,2,0:T(8,128)S(1)}, f32[2,64,8]{1,2,0:T(8,128)S(1)}, u32[]{:S(2)}, u32[]{:S(2)}) collective-permute-start(f32[2,64,8]{1,2,0:T(8,128)S(1)} %pad_maximum_fusion.27), channel_id=1, source_target_pairs={{1,0},{2,1},{3,2},{4,3},{5,4},{6,5},{7,6},{8,7},{9,8},{10,9},{11,1... | collective-permute-start | bytes 12296 | tf_op jit(solution)/shard_map/ppermute | solution.py:21
  215.5 6.8 %collective-permute-start.20 = (f32[2,64,128]{2,1,0:T(8,128)}, f32[2,64,128]{2,1,0:T(8,128)}, u32[]{:S(2)}, u32[]{:S(2)}) collective-permute-start(f32[2,64,128]{2,1,0:T(8,128)} %fusion.10), channel_id=1, source_target_pairs={{32,0},{64,32},{96,64},{128,96},{160,128},{192,160},{224,192},{33,... | collective-permute-start | bytes 196616 | tf_op jit(solution)/shard_map/ppermute | solution.py:21
  227.2 13.3 %collective-permute-start.22 = (f32[2,64,8]{1,2,0:T(8,128)S(1)}, f32[2,64,8]{1,2,0:T(8,128)S(1)}, u32[]{:S(2)}, u32[]{:S(2)}) collective-permute-start(f32[2,64,8]{1,2,0:T(8,128)S(1)} %pad_maximum_fusion.28), channel_id=1, source_target_pairs={{0,1},{1,2},{2,3},{3,4},{4,5},{5,6},{6,7},{7,8},{8,9},{9,10},{10,1... | collective-permute-start | bytes 12296 | tf_op jit(solution)/shard_map/ppermute | solution.py:21
  234.6 10.4 %collective-permute-start.23 = (f32[2,64,128]{2,1,0:T(8,128)}, f32[2,64,128]{2,1,0:T(8,128)}, u32[]{:S(2)}, u32[]{:S(2)}) collective-permute-start(f32[2,64,128]{2,1,0:T(8,128)} %fusion.9), channel_id=1, source_target_pairs={{0,32},{32,64},{64,96},{96,128},{128,160},{160,192},{192,224},{1,3... | collective-permute-start | bytes 196616 | tf_op jit(solution)/shard_map/ppermute | solution.py:21
  248.5 8.0 %collective-permute-start.25 = (f32[2,64,8]{1,2,0:T(8,128)S(1)}, f32[2,64,8]{1,2,0:T(8,128)S(1)}, u32[]{:S(2)}, u32[]{:S(2)}) collective-permute-start(f32[2,64,8]{1,2,0:T(8,128)S(1)} %pad_maximum_fusion.29), channel_id=1, source_target_pairs={{1,0},{2,1},{3,2},{4,3},{5,4},{6,5},{7,6},{8,7},{9,8},{10,9},{11,1... | collective-permute-start | bytes 12296 | tf_op jit(solution)/shard_map/ppermute | solution.py:21
  255.2 6.8 %collective-permute-start.24 = (f32[2,64,128]{2,1,0:T(8,128)}, f32[2,64,128]{2,1,0:T(8,128)}, u32[]{:S(2)}, u32[]{:S(2)}) collective-permute-start(f32[2,64,128]{2,1,0:T(8,128)} %bitcast.148), channel_id=1, source_target_pairs={{32,0},{64,32},{96,64},{128,96},{160,128},{192,160},{224,192},{33,... | collective-permute-start | bytes 196616 | tf_op jit(solution)/shard_map/ppermute | solution.py:21
  266.7 15.0 %collective-permute-start.26 = (f32[2,64,8]{1,2,0:T(8,128)S(1)}, f32[2,64,8]{1,2,0:T(8,128)S(1)}, u32[]{:S(2)}, u32[]{:S(2)}) collective-permute-start(f32[2,64,8]{1,2,0:T(8,128)S(1)} %pad_maximum_fusion.30), channel_id=1, source_target_pairs={{0,1},{1,2},{2,3},{3,4},{4,5},{5,6},{6,7},{7,8},{8,9},{9,10},{10,1... | collective-permute-start | bytes 12296 | tf_op jit(solution)/shard_map/ppermute | solution.py:21
  276.1 10.9 %collective-permute-start.27 = (f32[2,64,128]{2,1,0:T(8,128)}, f32[2,64,128]{2,1,0:T(8,128)}, u32[]{:S(2)}, u32[]{:S(2)}) collective-permute-start(f32[2,64,128]{2,1,0:T(8,128)} %fusion.8), channel_id=1, source_target_pairs={{0,32},{32,64},{64,96},{96,128},{128,160},{160,192},{192,224},{1,3... | collective-permute-start | bytes 196616 | tf_op jit(solution)/shard_map/ppermute | solution.py:21
  291.8 7.7 %collective-permute-start.29 = (f32[2,64,8]{1,2,0:T(8,128)S(1)}, f32[2,64,8]{1,2,0:T(8,128)S(1)}, u32[]{:S(2)}, u32[]{:S(2)}) collective-permute-start(f32[2,64,8]{1,2,0:T(8,128)S(1)} %pad_maximum_fusion.31), channel_id=1, source_target_pairs={{1,0},{2,1},{3,2},{4,3},{5,4},{6,5},{7,6},{8,7},{9,8},{10,9},{11,1... | collective-permute-start | bytes 12296 | tf_op jit(solution)/shard_map/ppermute | solution.py:21
  298.2 6.8 %collective-permute-start.28 = (f32[2,64,128]{2,1,0:T(8,128)}, f32[2,64,128]{2,1,0:T(8,128)}, u32[]{:S(2)}, u32[]{:S(2)}) collective-permute-start(f32[2,64,128]{2,1,0:T(8,128)} %fusion.7), channel_id=1, source_target_pairs={{32,0},{64,32},{96,64},{128,96},{160,128},{192,160},{224,192},{33,... | collective-permute-start | bytes 196616 | tf_op jit(solution)/shard_map/ppermute | solution.py:21
  308.6 14.3 %collective-permute-start.30 = (f32[2,64,8]{1,2,0:T(8,128)S(1)}, f32[2,64,8]{1,2,0:T(8,128)S(1)}, u32[]{:S(2)}, u32[]{:S(2)}) collective-permute-start(f32[2,64,8]{1,2,0:T(8,128)S(1)} %pad_maximum_fusion.32), channel_id=1, source_target_pairs={{0,1},{1,2},{2,3},{3,4},{4,5},{5,6},{6,7},{7,8},{8,9},{9,10},{10,1... | collective-permute-start | bytes 12296 | tf_op jit(solution)/shard_map/ppermute | solution.py:21
  316.5 8.9 %collective-permute-start.31 = (f32[2,64,128]{2,1,0:T(8,128)S(1)}, f32[2,64,128]{2,1,0:T(8,128)}, u32[]{:S(2)}, u32[]{:S(2)}) collective-permute-start(f32[2,64,128]{2,1,0:T(8,128)S(1)} %bitcast.520), channel_id=1, source_target_pairs={{0,32},{32,64},{64,96},{96,128},{128,160},{160,192},{192,224},{1,3... | collective-permute-start | bytes 196616 | tf_op jit(solution)/shard_map/ppermute | solution.py:21
  (111 other events, 889.0 us)
where the time goes:
time: 420 us; the launch traced here: 416 us
  starting transfers between devices  119 us (28%)
  local copies, waits for them, and re-layouts  106 us (25%)
  other arithmetic  98.7 us (24%)
  blocking collectives  80.6 us (19%)
  waiting for transfers between devices  7.37 us (2%)
    ppermute x32, starting transfers between devices, from_behind(): return lax.ppermute(block, axis, route)  112 us
    psum x5, blocking collectives, by_axis(): array = lax.psum(array, axis)  80.6 us
    slice x45, local copies, waits for them, and re-layouts, forward(): lax.slice_in_dim(field, 1, count, axis=axis)  33.4 us
    sub x8, other arithmetic, magnetic(): h_z = h_z - time_step * (ey_dx + psi_hzx - ex_dy - psi_hzy)  15.1 us
    sub x8, other arithmetic, magnetic(): h_x = h_x - time_step * (ez_dy + psi_hxy - ey_dz)  14.7 us
    another operation x24, local copies, waits for them, and re-layouts, forward(): jnp.expand_dims(plane, axis)  12.5 us
    sub x7, other arithmetic, magnetic(): h_y = h_y - time_step * (ex_dz - ez_dx - psi_hyx)  12 us
    add x6, other arithmetic, electric(): e_z = e_z + e_coef * (hy_dx + psi_ezx - hx_dy - psi_ezy)  10.3 us
  transfers between devices with their start and end apart: 33, of which 5 were waited for; matrix products, arithmetic and copies ran while one was open for 38% of the time, Pallas kernels for 0%

commit v1 on v0

v1 whole, which is shorter than its diff:
```python
import functools

import jax
import jax.numpy as jnp
from jax import lax
from jax.experimental import pallas as pl
from jax.experimental.pallas import tpu as pltpu
from jax.sharding import Mesh
from jax.sharding import PartitionSpec as P

STEPS = 8
ROW = ("row_0", "row_1")
COL = ("col_0", "col_1", "col_2")
NEAR = ("row_1", "col_1", "col_2")
FAR = ("row_0", "col_0")

time_step = 0.5
sigma_top = 4.0
alpha_shift = 0.05

NZ = 64
HALF = 64
ROWS = HALF + 2 * STEPS
TILES = ROWS // 8
SENT = ROWS - 8
DEEP = STEPS // 2


def tile(t, shift=0):
    return slice(8 + 8 * t + shift, 16 + 8 * t + shift)


def lanes():
    return lax.broadcasted_iota(jnp.int32, (8, 128), 1)


def swap(block):
    return pltpu.roll(block, 64, 1)


def prepare(e_ref, h_ref, c_ref, t_ref, up_ref, down_ref):
    for comp in range(7):
        src, at = ((e_ref, comp) if comp < 3 else (h_ref, comp - 3)) if comp < 6 else (c_ref, 0)
        for j in range(4):
            block = jnp.concatenate(
                [src[at, pl.ds(j, NZ, stride=8), :], src[at, pl.ds(j + 4, NZ, stride=8), :]], 0
            )
            turned = block.T
            up_ref[comp, j] = turned[120:128]
            down_ref[comp, j] = turned[0:8]
            low = lanes() < 64
            for k in range(8):
                first, second = turned[8 * k : 8 * k + 8], turned[64 + 8 * k : 72 + 8 * k]
                t_ref[comp, j, 8 + 8 * k : 16 + 8 * k] = jnp.where(low, first, swap(second))
                t_ref[comp, j + 4, 8 + 8 * k : 16 + 8 * k] = jnp.where(low, swap(first), second)
            before, after = turned[56:64], turned[64:72]
            t_ref[comp, j, 0:8] = swap(before)
            t_ref[comp, j + 4, 0:8] = before
            t_ref[comp, j, 72:80] = after
            t_ref[comp, j + 4, 72:80] = swap(after)


def merge(t_ref, below_ref, above_ref, comp, col, last, write):
    low = lanes() < 64
    for x in range(8):
        for t in range(TILES):
            value = t_ref[comp, x, 8 * t : 8 * t + 8]
            if t == 0:
                halo = below_ref[comp, x % 4]
                halo = swap(halo) if x >= 4 else halo
                value = jnp.where(low, jnp.where(col > 0, halo, 0.0), value)
            if t == TILES - 1:
                halo = above_ref[comp, x % 4]
                halo = swap(halo) if x < 4 else halo
                value = jnp.where(low, value, jnp.where(col < last, halo, 0.0))
            write(x, t, value)


def absorber(positions, total, low, high):
    depth = jnp.maximum(
        jnp.maximum((low - positions) / low, (positions - (total - 1.0 - high)) / high), 0.0
    )
    sigma = sigma_top * depth**3
    damp = jnp.exp(-(sigma + alpha_shift) * time_step)
    gain = sigma / (sigma + alpha_shift) * (damp - 1.0)
    return (damp, gain)


def tables(sc_ref, xt_ref, yt_ref, hc_ref, planes, full_x, full_y):
    widths = [sc_ref[i].astype(jnp.float32) for i in range(4)]
    row, col = sc_ref[4], sc_ref[5]
    for p, x in planes:
        at = jnp.full((8, 128), (row * 8 + x).astype(jnp.float32))
        for k, shift in ((0, 0.5), (2, 0.0)):
            damp, gain = absorber(at + shift, float(full_x), widths[0], widths[1])
            xt_ref[k, p] = damp
            xt_ref[k + 1, p] = gain
    for t in range(TILES):
        half = jnp.where(lanes() < 64, 0, 64)
        y = col * 128 + half + 8 * t - STEPS + lax.broadcasted_iota(jnp.int32, (8, 128), 0)
        at = y.astype(jnp.float32)
        for k, shift in ((0, 0.5), (2, 0.0)):
            damp, gain = absorber(at + shift, float(full_y), widths[2], widths[3])
            yt_ref[k, 8 * t : 8 * t + 8] = damp
            yt_ref[k + 1, 8 * t : 8 * t + 8] = gain
        step = jnp.where(y >= 0, time_step, 0.0)
        hc_ref[0, 8 * t : 8 * t + 8] = step
        hc_ref[1, 8 * t : 8 * t + 8] = jnp.where(row > 0, step, 0.0)


def magnetic(f, psi, p, xt, yt, hc, which):
    z_last = (lanes() & 63) == 63
    damp_x, gain_x = xt[0, p], xt[1, p]
    for t in range(TILES):
        here, rows = tile(t), slice(8 * t, 8 * t + 8)
        e_x, e_y, e_z = f[0, p, here], f[1, p, here], f[2, p, here]
        ez_dy = f[2, p, tile(t, 1)] - e_z
        ex_dy = f[0, p, tile(t, 1)] - e_x
        ey_dz = jnp.where(z_last, 0.0, pltpu.roll(e_y, 127, 1)) - e_y
        ex_dz = jnp.where(z_last, 0.0, pltpu.roll(e_x, 127, 1)) - e_x
        ez_dx = f[2, p + 1, here] - e_z
        ey_dx = f[1, p + 1, here] - e_y
        damp_y, gain_y, step = yt[0, rows], yt[1, rows], hc[which, rows]
        psi_hxy = damp_y * psi[0, p, rows] + gain_y * ez_dy
        psi_hyx = damp_x * psi[1, p, rows] + gain_x * ez_dx
        psi_hzx = damp_x * psi[2, p, rows] + gain_x * ey_dx
        psi_hzy = damp_y * psi[3, p, rows] + gain_y * ex_dy
        psi[0, p, rows] = psi_hxy
        psi[1, p, rows] = psi_hyx
        psi[2, p, rows] = psi_hzx
        psi[3, p, rows] = psi_hzy
        f[3, p, here] = f[3, p, here] - step * (ez_dy + psi_hxy - ey_dz)
        f[4, p, here] = f[4, p, here] - step * (ex_dz - ez_dx - psi_hyx)
        f[5, p, here] = f[5, p, here] - step * (ey_dx + psi_hzx - ex_dy - psi_hzy)


def electric(f, psi, coef, p, xt, yt):
    z_first = (lanes() & 63) == 0
    damp_x, gain_x = xt[2, p], xt[3, p]
    for t in range(TILES):
        here, rows = tile(t), slice(8 * t, 8 * t + 8)
        h_x, h_y, h_z = f[3, p, here], f[4, p, here], f[5, p, here]
        hz_dy = h_z - f[5, p, tile(t, -1)]
        hx_dy = h_x - f[3, p, tile(t, -1)]
        hy_dz = h_y - jnp.where(z_first, 0.0, pltpu.roll(h_y, 1, 1))
        hx_dz = h_x - jnp.where(z_first, 0.0, pltpu.roll(h_x, 1, 1))
        hz_dx = h_z - f[5, p - 1, here]
        hy_dx = h_y - f[4, p - 1, here]
        damp_y, gain_y, step = yt[2, rows], yt[3, rows], coef[p, rows]
        psi_exy = damp_y * psi[4, p, rows] + gain_y * hz_dy
        psi_eyx = damp_x * psi[5, p, rows] + gain_x * hz_dx
        psi_ezx = damp_x * psi[6, p, rows] + gain_x * hy_dx
        psi_ezy = damp_y * psi[7, p, rows] + gain_y * hx_dy
        psi[4, p, rows] = psi_exy
        psi[5, p, rows] = psi_eyx
        psi[6, p, rows] = psi_ezx
        psi[7, p, rows] = psi_ezy
        f[0, p, here] = f[0, p, here] + step * (hz_dy + psi_exy - hy_dz)
        f[1, p, here] = f[1, p, here] + step * (hx_dz - hz_dx - psi_eyx)
        f[2, p, here] = f[2, p, here] + step * (hy_dx + psi_ezx - hx_dy - psi_ezy)


def pack(read, out_ref, at):
    low = lanes() < 64
    for t in range(TILES - 1):
        out_ref[at, 8 * t : 8 * t + 8] = jnp.where(low, read(t), read(t + 1))


def unpack(ref, at, t):
    low = lanes() < 64
    first = ref[at, 8 * t : 8 * t + 8] if t < TILES - 1 else swap(ref[at, 0:8])
    second = ref[at, 8 * t - 8 : 8 * t] if t > 0 else swap(ref[at, SENT - 8 : SENT])
    return jnp.where(low, first, second)


def zero_planes(ref, comps, planes, rows):
    zero = jnp.zeros((rows, 128), jnp.float32)

    def one(p, carry):
        for c in comps:
            ref[c, p] = zero
        return carry

    lax.fori_loop(planes[0], planes[1], one, 0)


def alone(full_x, full_y, last, sc, t_ref, below, above, up_ref, down_ref, f, psi, coef, xt, yt, hc):
    col = sc[5]
    tables(sc, xt, yt, hc, [(1 + x, x) for x in range(8)], full_x, full_y)
    zero_planes(f, range(6), (0, 10), ROWS + 16)
    zero_planes(psi, range(8), (1, 9), ROWS)
    for comp in range(6):

        def write(x, t, value, comp=comp):
            f[comp, 1 + x, tile(t)] = value

        merge(t_ref, below, above, comp, col, last, write)

    def write_coef(x, t, value):
        coef[1 + x, 8 * t : 8 * t + 8] = value

    merge(t_ref, below, above, 6, col, last, write_coef)
    for k in range(DEEP):
        pack(lambda t: coef[5 + k, 8 * t : 8 * t + 8], up_ref, 2 * STEPS + k)
        pack(lambda t: coef[1 + k, 8 * t : 8 * t + 8], down_ref, 2 * STEPS + k)

    def step(s, carry):
        for c in range(2):
            pack(lambda t: f[1 + c, 1, tile(t)], down_ref, 2 * s + c)

        def h_pair(i, carry):
            for k in range(4):
                magnetic(f, psi, 1 + 4 * i + k, xt, yt, hc, 0)
            return carry

        def e_pair(i, carry):
            for k in range(4):
                electric(f, psi, coef, 1 + 4 * i + k, xt, yt)
            return carry

        lax.fori_loop(0, 2, h_pair, 0)
        for c in range(2):
            pack(lambda t: f[4 + c, 8, tile(t)], up_ref, 2 * s + c)
        lax.fori_loop(0, 2, e_pair, 0)
        return carry

    lax.fori_loop(0, STEPS, step, 0)


def joined(
    full_x, full_y, last_row, last, count, sc, snap, t_ref, below, above, left_ref, right_ref, modes_ref,
    out_ref, e_out, h_out, f, psi, coef, xt, yt, hc, planes, snaps, gram_ref, sems,
):
    row, col = sc[4], sc[5]
    cells = [(1 + k, k - 4) for k in range(4)] + [(6 + x, x) for x in range(8)]
    cells = cells + [(15 + k, 8 + k) for k in range(4)]
    tables(sc, xt, yt, hc, cells, full_x, full_y)
    zero_planes(f, range(6), (0, 20), ROWS + 16)
    zero_planes(psi, range(8), (1, 19), ROWS)
    for comp in range(6):

        def write(x, t, value, comp=comp):
            f[comp, 6 + x, tile(t)] = value

        merge(t_ref, below, above, comp, col, last, write)

    def write_coef(x, t, value):
        coef[6 + x, 8 * t : 8 * t + 8] = value

    merge(t_ref, below, above, 6, col, last, write_coef)
    for k in range(DEEP):
        for t in range(TILES):
            rows = slice(8 * t, 8 * t + 8)
            coef[1 + k, rows] = jnp.where(row > 0, unpack(left_ref, 2 * STEPS + k, t), 0.0)
            coef[15 + k, rows] = jnp.where(row < last_row, unpack(right_ref, 2 * STEPS + k, t), 0.0)

    def step(s, carry):
        deep = jnp.minimum(s + 1, STEPS - s)
        for c in range(2):
            for t in range(TILES):
                here = tile(t)
                came = jnp.where(row < last_row, unpack(right_ref, 2 * s + c, t), 0.0)
                f[1 + c, 14, here] = f[1 + c, 15, here] + came
                f[1 + c, 5, here] = f[1 + c, 6, here]

        def h_main(i, carry):
            for k in range(4):
                magnetic(f, psi, 6 + 4 * i + k, xt, yt, hc, 0)
            return carry

        def h_side(k, carry):
            magnetic(f, psi, 4 - k, xt, yt, hc, 1)
            magnetic(f, psi, 15 + k, xt, yt, hc, 0)
            return carry

        def e_main(i, carry):
            for k in range(4):
                electric(f, psi, coef, 6 + 4 * i + k, xt, yt)
            return carry

        def e_side(k, carry):
            electric(f, psi, coef, 4 - k, xt, yt)
            electric(f, psi, coef, 15 + k, xt, yt)
            return carry

        lax.fori_loop(0, 2, h_main, 0)
        lax.fori_loop(0, deep, h_side, 0)
        for c in range(2):
            for t in range(TILES):
                here = tile(t)
                came = jnp.where(row > 0, unpack(left_ref, 2 * s + c, t), 0.0)
                f[4 + c, 5, here] = f[4 + c, 4, here] + came
                f[4 + c, 14, here] = f[4 + c, 13, here]
        lax.fori_loop(0, 2, e_main, 0)
        lax.fori_loop(0, deep, e_side, 0)
        return carry

    lax.fori_loop(0, STEPS, step, 0)

    low = lax.broadcasted_iota(jnp.int32, (HALF, 128), 1) < 64
    own = slice(8 + STEPS, 8 + STEPS + HALF)
    for comp in range(6):
        for j in range(4):
            first, second = f[comp, 6 + j, own], f[comp, 10 + j, own]
            top = jnp.where(low, first, swap(second))
            bottom = jnp.where(low, swap(first), second)
            turned = jnp.concatenate([top, bottom], 0).T
            planes[pl.ds(comp * 8 * NZ + j, NZ, stride=8), :] = turned[:NZ]
            planes[pl.ds(comp * 8 * NZ + j + 4, NZ, stride=8), :] = turned[NZ:]
    size = 3 * NZ * 8
    copies = [
        pltpu.make_async_copy(planes.at[pl.ds(0, size)], e_out, sems.at[0]),
        pltpu.make_async_copy(planes.at[pl.ds(size, size)], h_out, sems.at[1]),
    ]
    for copy in copies:
        copy.start()
    for s in range(count):
        snaps[8 * s : 8 * s + 8] = planes[pl.ds(pl.multiple_of(snap[s] * 8, 8), 8), :]
    gram = jnp.zeros((count, count), jnp.float32)
    coefficients = jnp.zeros((count, 128), jnp.float32)
    contract = functools.partial(
        lax.dot_general,
        dimension_numbers=(((1,), (1,)), ((), ())),
        precision=lax.Precision.HIGHEST,
        preferred_element_type=jnp.float32,
    )
    for x in range(8):
        part = snaps[pl.ds(x, count, stride=8), :]
        gram = gram + contract(part, part)
        coefficients = coefficients + contract(part, modes_ref[pl.ds(x, 128, stride=8), :])
    gram_ref[...] = jnp.concatenate([gram[:32], gram[32:]], 1) / float(full_x * full_y)
    for b in range(8):
        out_ref[b, 0:8] = coefficients[8 * b : 8 * b + 8]
        out_ref[b, 8:12] = gram_ref[4 * b : 4 * b + 4]
    for copy in copies:
        copy.wait()


def around(block, axis, distance):
    size = lax.axis_size(axis)
    return lax.ppermute(block, axis, [(i, (i + distance) % size) for i in range(size)])


def spread(block, axes, size):
    whole = jnp.broadcast_to(block, (size,) + block.shape)
    return lax.all_to_all(whole, axes, split_axis=0, concat_axis=0, tiled=True)


def f32(*shape):
    return jax.ShapeDtypeStruct(shape, jnp.float32)


def shards(e_field, h_field, e_coef, basis, pml_width, snap_index):
    rows_count, cols_count = lax.axis_size(ROW), lax.axis_size(COL)
    full_x, full_y = 8 * rows_count, 128 * cols_count
    row, col = lax.axis_index(ROW), lax.axis_index(COL)
    count = snap_index.shape[0]
    scalars = jnp.concatenate([pml_width, jnp.stack([row, col]).astype(jnp.int32)])
    vmem = pl.BlockSpec(memory_space=pltpu.VMEM)
    smem = pl.BlockSpec(memory_space=pltpu.SMEM)
    params = pltpu.CompilerParams(vmem_limit_bytes=56 * 1024 * 1024)

    local_modes = lax.all_to_all(basis, ROW, split_axis=1, concat_axis=0, tiled=True)

    turned, up, down = pl.pallas_call(
        prepare,
        out_shape=(f32(7, 8, ROWS, 128), f32(7, 4, 8, 128), f32(7, 4, 8, 128)),
        in_specs=[vmem] * 3,
        out_specs=(vmem,) * 3,
        compiler_params=params,
    )(e_field.reshape(3, 512, 128), h_field.reshape(3, 512, 128), e_coef.reshape(1, 512, 128))
    below, above = around(up, COL, 1), around(down, COL, -1)

    def scratch(planes):
        return [
            pltpu.VMEM((6, planes, ROWS + 16, 128), jnp.float32),
            pltpu.VMEM((8, planes, ROWS, 128), jnp.float32),
            pltpu.VMEM((planes, ROWS, 128), jnp.float32),
            pltpu.VMEM((4, planes, 8, 128), jnp.float32),
            pltpu.VMEM((4, ROWS, 128), jnp.float32),
            pltpu.VMEM((2, ROWS, 128), jnp.float32),
        ]

    sent = f32(2 * STEPS + DEEP, SENT, 128)
    up, down = pl.pallas_call(
        functools.partial(alone, full_x, full_y, cols_count - 1),
        out_shape=(sent, sent),
        in_specs=[smem] + [vmem] * 3,
        out_specs=(vmem,) * 2,
        scratch_shapes=scratch(10),
        compiler_params=params,
    )(scalars, turned, below, above)
    left, right = around(up, ROW, 1), around(down, ROW, -1)

    anywhere = pl.BlockSpec(memory_space=pl.ANY)
    sums, e_final, h_final = pl.pallas_call(
        functools.partial(joined, full_x, full_y, rows_count - 1, cols_count - 1, count),
        out_shape=(f32(8, 12, 128), f32(1536, 128), f32(1536, 128)),
        in_specs=[smem] * 2 + [vmem] * 6,
        out_specs=(vmem, anywhere, anywhere),
        scratch_shapes=scratch(20)
        + [
            pltpu.VMEM((6 * NZ * 8, 128), jnp.float32),
            pltpu.VMEM((count * 8, 128), jnp.float32),
            pltpu.VMEM((32, 128), jnp.float32),
            pltpu.SemaphoreType.DMA((2,)),
        ],
        compiler_params=params,
    )(scalars, snap_index, turned, below, above, left, right, local_modes.reshape(1024, 128))

    part = lax.all_to_all(sums, NEAR, split_axis=0, concat_axis=0, tiled=True).sum(0)
    part = spread(part, FAR, lax.axis_size(FAR)).sum(0)
    whole = spread(part, NEAR, lax.axis_size(NEAR))
    coefficients = whole[:, :8].reshape(count, 128)
    packed = whole[:, 8:].reshape(count // 2, 128)
    gram = jnp.concatenate([packed[:, :64], packed[:, 64:]], 0)
    shape = e_field.shape
    return (e_final.reshape(shape), h_final.reshape(shape), coefficients, gram)


def solution(mesh):
    split = Mesh(mesh.devices.reshape(4, 2, 8, 2, 2), ROW + COL)
    return jax.shard_map(
        shards,
        mesh=split,
        in_specs=(
            P(None, None, ROW, COL),
            P(None, None, ROW, COL),
            P(None, ROW, COL),
            P(ROW, None, COL),
            P(),
            P(),
        ),
        out_specs=(P(None, None, ROW, COL), P(None, None, ROW, COL), P(), P()),
        check_vma=False,
    )
```

time: 420 us -> 135 us (0.32)
  starting transfers between devices: 119 us -> 8.28 us
  local copies, waits for them, and re-layouts: 106 us -> 3.77 us
  other arithmetic: 98.7 us -> 1.88 us
  Pallas kernels: 0 us -> 39.1 us
  waiting for transfers between devices: 7.37 us -> 2.69 us
    ppermute x32 -> x4, starting transfers between devices: 112 us -> 8.28 us  [around(): lax.ppermute(block, axis, [(i, (i + distance) % size) for i in range(size)])]
    psum x5 -> x0, blocking collectives: 80.6 us -> none  [by_axis(): array = lax.psum(array, axis)]
    all_to_all x0 -> x4, blocking collectives: none -> 78.4 us  [the longest x1 38.3 us: shards(): lax.all_to_all(basis, ROW, split_axis=1, concat_axis=0, tiled=True)]
    slice x123 -> x2, local copies, waits for them, and re-layouts: 71.1 us -> 0.08 us  [the longest x1 0.07 us: shards(): gram = jnp.concatenate([packed[:, :64], packed[:, 64:]], 0)]
    sub x23 -> x0, other arithmetic: 41.8 us -> none  [the longest x8 15.1 us: magnetic(): h_z = h_z - time_step * (ey_dx + psi_hzx - ex_dy - psi_hzy)]
    pallas_call x0 -> x3, Pallas kernels: none -> 39.1 us  [the longest x1 25.1 us: shards(): pl.pallas_call(functools.partial(joined, full_x, full_y, rows_count - 1,...]
    add x20 -> x0, other arithmetic: 25.6 us -> none  [the longest x6 10.3 us: electric(): e_z = e_z + e_coef * (hy_dx + psi_ezx - hx_dy - psi_ezy)]
    another operation x68 -> x0, local copies, waits for them, and re-layouts: 25.4 us -> none  [the longest x24 12.5 us: forward(): jnp.expand_dims(plane, axis)]
  transfers between devices with their start and end apart: 33 -> 4, of which waited for: 5 -> 2; matrix products, arithmetic and copies ran while one was open for 38% -> 2% of each run, Pallas kernels for 0% -> 0%
where the time goes in v1:
time: 135 us
  blocking collectives  78.4 us (58%)
  Pallas kernels  39.1 us (29%)
  starting transfers between devices  8.28 us (6%)
  local copies, waits for them, and re-layouts  3.77 us (3%)
  waiting for transfers between devices  2.69 us (2%)
  other arithmetic  1.88 us (1%)
    all_to_all x1, blocking collectives, shards(): lax.all_to_all(basis, ROW, split_axis=1, concat_axis=0, tiled=True)  38.3 us
    all_to_all x2, blocking collectives, spread(): return lax.all_to_all(whole, axes, split_axis=0, concat_axis=0, tiled=True)  31.5 us
    pallas_call x1, Pallas kernels, shards(): pl.pallas_call(functools.partial(joined, full_x, full_y, rows_count - 1,...  25.1 us
    pallas_call x1, Pallas kernels, shards(): pl.pallas_call(functools.partial(alone, full_x, full_y, cols_count - 1),...  10 us
    all_to_all x1, blocking collectives, shards(): lax.all_to_all(sums, NEAR, split_axis=0, concat_axis=0, tiled=True).sum(0)  8.6 us
    ppermute x4, starting transfers between devices, around(): lax.ppermute(block, axis, [(i, (i + distance) % size) for i in range(size)])  8.28 us
    pallas_call x1, Pallas kernels, shards(): pl.pallas_call(prepare, out_shape=(f32(7, 8, ROWS, 128), f32(7, 4, 8, 128...  3.96 us
  transfers between devices with their start and end apart: 4, of which 2 were waited for; matrix products, arithmetic and copies ran while one was open for 2% of the time, Pallas kernels for 0%

profile of v1, /device:TPU:1, one launch (start us, length us, event | category | flops | bytes accessed | tf_op | source)
XLA Modules:
  0.0 134.8 jit_solution(5794672351749976075)
XLA Ops:
  0.6 0.0 copy-start.2
  0.6 4.0 %shard_map.93 = (f32[7,8,80,128]{3,2,1,0:T(8,128)}, f32[7,4,8,128]{3,2,1,0:T(8,128)}, f32[7,4,8,128]{3,2,1,0:T(8,128)}) custom-call(f32[3,512,128]{2,1,0:T(8,128)} %bitcast.16, f32[3,512,128]{2,1,0:T(8,128)} %bitcast.17, f32[1,512,128]{2,1,0:T(8,128)} %bitcast.18), custom_call_target="tpu_custom_call" | custom-call | tf_op jit(solution)/shard_map/pallas_call | solution.py:365
  4.6 2.7 %collective-permute-start = (f32[7,4,8,128]{3,2,1,0:T(8,128)}, f32[7,4,8,128]{3,2,1,0:T(8,128)S(1)}, u32[]{:S(2)}, u32[]{:S(2)}) collective-permute-start(f32[7,4,8,128]{3,2,1,0:T(8,128)} %get-tuple-element.13), channel_id=1, source_target_pairs={{0,1},{1,2},{2,3},{3,4},{4,5},{5,6},{6,7},{7,8},{8,9},{9,10},{10,1... | collective-permute-start | bytes 344072 | tf_op jit(solution)/shard_map/ppermute | solution.py:341
  7.3 0.5 collective-permute-start.1
  7.8 1.2 pad_add_fusion.sc
  9.0 0.4 collective-permute-done.below
  9.4 0.0 copy-start.3
  9.4 2.3 %collective-permute-done.1.above = f32[7,4,8,128]{3,2,1,0:T(8,128)S(1)} collective-permute-done((f32[7,4,8,128]{3,2,1,0:T(8,128)}, f32[7,4,8,128]{3,2,1,0:T(8,128)S(1)}, u32[]{:S(2)}, u32[]{:S(2)}) %collective-permute-start.1) | collective-permute-done | bytes 114720 | tf_op jit(solution)/shard_map/ppermute | solution.py:341
  11.7 0.0 copy-start.4
  11.7 0.0 copy-done.3
  11.7 0.6 copy-done.4
  12.3 10.0 %shard_map.94 = (f32[20,72,128]{2,1,0:T(8,128)}, f32[20,72,128]{2,1,0:T(8,128)}) custom-call(s32[6]{0:T(128)} %pad_add_fusion.sc, f32[7,8,80,128]{3,2,1,0:T(8,128)} %get-tuple-element.12.t_ref, f32[7,4,8,128]{3,2,1,0:T(8,128)} %copy-done.3, f32[7,4,8,128]{3,2,1,0:T(8,128)} %copy-done.4), custom_call_target="tpu_custom_call" | custom-call | tf_op jit(solution)/shard_map/pallas_call | solution.py:385
  22.4 2.6 %collective-permute-start.2 = (f32[20,72,128]{2,1,0:T(8,128)}, f32[20,72,128]{2,1,0:T(8,128)S(1)}, u32[]{:S(2)}, u32[]{:S(2)}) collective-permute-start(f32[20,72,128]{2,1,0:T(8,128)} %get-tuple-element.15), channel_id=1, source_target_pairs={{0,32},{32,64},{64,96},{96,128},{128,160},{160,192},{192,224},{224... | collective-permute-start | bytes 2211848 | tf_op jit(solution)/shard_map/ppermute | solution.py:341
  25.0 2.5 %collective-permute-start.3 = (f32[20,72,128]{2,1,0:T(8,128)}, f32[20,72,128]{2,1,0:T(8,128)S(1)}, u32[]{:S(2)}, u32[]{:S(2)}) collective-permute-start(f32[20,72,128]{2,1,0:T(8,128)} %get-tuple-element.16), channel_id=1, source_target_pairs={{0,224},{32,0},{64,32},{96,64},{128,96},{160,128},{192,160},{224,1... | collective-permute-start | bytes 2211848 | tf_op jit(solution)/shard_map/ppermute | solution.py:341
  27.5 0.0 copy-done.2
  27.5 0.3 copy.15
  27.8 38.3 %all_to_all.30 = f32[16,64,128]{2,0,1:T(8,128)S(1)} all-to-all(f32[16,64,128]{2,0,1:T(8,128)S(1)} %copy.15), channel_id=1, replica_groups=mesh['row_0'=4,'row_1'=2,'col_0'=8,'col_1'=2,'col_2'=2] {'row_0','row_1'}, dimensions={1} | all-to-all | bytes 1048576 | tf_op jit(solution)/shard_map/all_to_all | solution.py:363
  66.0 0.9 copy.16
  67.0 0.0 collective-permute-done.2.left_ref
  67.0 0.0 copy-start
  67.0 0.0 collective-permute-done.3.right_ref
  67.0 0.0 copy-start.1
  67.0 0.9 copy-done
  67.9 0.3 copy-done.1
  68.1 25.1 %shard_map.95 = (f32[8,12,128]{2,1,0:T(8,128)}, f32[1536,128]{1,0:T(8,128)}, f32[1536,128]{1,0:T(8,128)}) custom-call(s32[6]{0:T(128)} %pad_add_fusion.sc, s32[64]{0:T(128)} %snap.1, f32[7,8,80,128]{3,2,1,0:T(8,128)} %get-tuple-element.12.t_ref, f32[7,4,8,128]{3,2,1,0:T(8,128)} %copy-done.3, f32[7,4,8,128]{3,2,1,0:T(8,128)} %copy-done.4, ...), custom_call_target="tpu_custom_call" | custom-call | tf_op jit(solution)/shard_map/pallas_call | solution.py:396
  93.3 8.6 %all_to_all.31 = f32[8,12,128]{2,1,0:T(8,128)S(1)} all-to-all(f32[8,12,128]{2,1,0:T(8,128)} %get-tuple-element.19), channel_id=1, replica_groups=mesh['row_0'=4,'row_1'=2,'col_0'=8,'col_1'=2,'col_2'=2] {'row_1','col_1'..., dimensions={0} | all-to-all | bytes 98304 | tf_op jit(solution)/shard_map/all_to_all | solution.py:411
  101.9 20.5 %all_to_all.32 = f32[32,12,128]{2,1,0:T(8,128)S(1)} all-to-all(f32[32,12,128]{2,1,0:T(8,128)S(1)} %broadcast_in_dim.6), channel_id=1, replica_groups=mesh['row_0'=4,'row_1'=2,'col_0'=8,'col_1'=2,'col_2'=2] {'row_0','col_0'}, dimensions={0} | all-to-all | bytes 393216 | tf_op jit(solution)/shard_map/all_to_all | solution.py:346
  122.5 11.0 %all_to_all.33 = f32[8,12,128]{2,1,0:T(8,128)S(1)} all-to-all(f32[8,12,128]{2,1,0:T(8,128)S(1)} %broadcast_in_dim.7), channel_id=1, replica_groups=mesh['row_0'=4,'row_1'=2,'col_0'=8,'col_1'=2,'col_2'=2] {'row_1','col_1'..., dimensions={0} | all-to-all | bytes 98304 | tf_op jit(solution)/shard_map/all_to_all | solution.py:346
  133.5 0.1 fusion
  133.6 0.6 pad_maximum_fusion
  134.2 0.6 slice_bitcast_fusion
  (5 shorter events, 0.1 us)
Async XLA Ops:
  0.6 26.8 %copy-start.2 = (f32[16,64,128]{2,1,0:T(8,128)S(1)}, f32[16,64,128]{2,1,0:T(8,128)}, u32[]{:S(2)}) copy-start(f32[16,64,128]{2,1,0:T(8,128)} %param.9) | copy-start | bytes 1572868
  4.6 4.8 %collective-permute-start = (f32[7,4,8,128]{3,2,1,0:T(8,128)}, f32[7,4,8,128]{3,2,1,0:T(8,128)S(1)}, u32[]{:S(2)}, u32[]{:S(2)}) collective-permute-start(f32[7,4,8,128]{3,2,1,0:T(8,128)} %get-tuple-element.13), channel_id=1, source_target_pairs={{0,1},{1,2},{2,3},{3,4},{4,5},{5,6},{6,7},{7,8},{8,9},{9,10},{10,1... | collective-permute-start | bytes 344072 | tf_op jit(solution)/shard_map/ppermute | solution.py:341
  7.3 4.4 %collective-permute-start.1 = (f32[7,4,8,128]{3,2,1,0:T(8,128)}, f32[7,4,8,128]{3,2,1,0:T(8,128)S(1)}, u32[]{:S(2)}, u32[]{:S(2)}) collective-permute-start(f32[7,4,8,128]{3,2,1,0:T(8,128)} %get-tuple-element.14), channel_id=1, source_target_pairs={{0,31},{1,0},{2,1},{3,2},{4,3},{5,4},{6,5},{7,6},{8,7},{9,8},{10,9... | collective-permute-start | bytes 344072 | tf_op jit(solution)/shard_map/ppermute | solution.py:341
  9.4 2.3 %copy-start.3 = (f32[7,4,8,128]{3,2,1,0:T(8,128)}, f32[7,4,8,128]{3,2,1,0:T(8,128)S(1)}, u32[]{:S(2)}) copy-start(f32[7,4,8,128]{3,2,1,0:T(8,128)S(1)} %collective-permute-done.below) | copy-start | bytes 344068
  11.7 0.6 copy-start.4
  22.4 44.6 %collective-permute-start.2 = (f32[20,72,128]{2,1,0:T(8,128)}, f32[20,72,128]{2,1,0:T(8,128)S(1)}, u32[]{:S(2)}, u32[]{:S(2)}) collective-permute-start(f32[20,72,128]{2,1,0:T(8,128)} %get-tuple-element.15), channel_id=1, source_target_pairs={{0,32},{32,64},{64,96},{96,128},{128,160},{160,192},{192,224},{224... | collective-permute-start | bytes 2211848 | tf_op jit(solution)/shard_map/ppermute | solution.py:341
  25.0 42.0 %collective-permute-start.3 = (f32[20,72,128]{2,1,0:T(8,128)}, f32[20,72,128]{2,1,0:T(8,128)S(1)}, u32[]{:S(2)}, u32[]{:S(2)}) collective-permute-start(f32[20,72,128]{2,1,0:T(8,128)} %get-tuple-element.16), channel_id=1, source_target_pairs={{0,224},{32,0},{64,32},{96,64},{128,96},{160,128},{192,160},{224,1... | collective-permute-start | bytes 2211848 | tf_op jit(solution)/shard_map/ppermute | solution.py:341
  67.0 0.9 copy-start
  67.0 1.1 copy-start.1

commit v2 on v1

v2 whole, which is shorter than its diff:
```python
import functools

import jax
import jax.numpy as jnp
from jax import lax
from jax.experimental import pallas as pl
from jax.experimental.pallas import tpu as pltpu
from jax.sharding import Mesh
from jax.sharding import PartitionSpec as P

STEPS = 8
ROW = ("row_0", "row_1")
COL = ("col_0", "col_1", "col_2")
NEAR = ("row_1", "col_1", "col_2")
FAR = ("row_0", "col_0")

time_step = 0.5
sigma_top = 4.0
alpha_shift = 0.05

NZ = 64
HALF = 64
ROWS = HALF + 2 * STEPS
TILES = ROWS // 8
SENT = ROWS - 8
DEEP = STEPS // 2


def tile(t, shift=0):
    return slice(8 + 8 * t + shift, 16 + 8 * t + shift)


def lanes():
    return lax.broadcasted_iota(jnp.int32, (8, 128), 1)


def swap(block):
    return pltpu.roll(block, 64, 1)


def prepare(e_hbm, h_hbm, c_hbm, t_hbm, up_ref, down_ref, cup_ref, cdown_ref, src, t_ref, sems):
    comes = []
    for comp in range(7):
        ref, at = ((e_hbm, comp) if comp < 3 else (h_hbm, comp - 3)) if comp < 6 else (c_hbm, 0)
        comes.append(pltpu.make_async_copy(ref.at[at], src.at[comp], sems.at[comp]))
        comes[comp].start()
    goes = []
    for comp in range(7):
        comes[comp].wait()
        for j in range(4):
            block = jnp.concatenate(
                [src[comp, pl.ds(j, NZ, stride=8), :], src[comp, pl.ds(j + 4, NZ, stride=8), :]], 0
            )
            turned = block.T
            up_ref[comp, j] = turned[120:128]
            down_ref[comp, j] = turned[0:8]
            low = lanes() < 64
            for k in range(8):
                first, second = turned[8 * k : 8 * k + 8], turned[64 + 8 * k : 72 + 8 * k]
                first, second = jnp.where(low, first, swap(second)), jnp.where(low, swap(first), second)
                t_ref[comp, j, 8 + 8 * k : 16 + 8 * k] = first
                t_ref[comp, j + 4, 8 + 8 * k : 16 + 8 * k] = second
                if comp == 6:
                    cdown_ref[j, 8 * k : 8 * k + 8] = first
                    cup_ref[j, 8 * k : 8 * k + 8] = second
            before, after = turned[56:64], turned[64:72]
            t_ref[comp, j, 0:8] = swap(before)
            t_ref[comp, j + 4, 0:8] = before
            t_ref[comp, j, 72:80] = after
            t_ref[comp, j + 4, 72:80] = swap(after)
        goes.append(pltpu.make_async_copy(t_ref.at[comp], t_hbm.at[comp], sems.at[7 + comp]))
        goes[comp].start()
    for go in goes:
        go.wait()


def fill(f, coef, t_hbm, below_hbm, above_hbm, halo, sems, first):
    copies = []
    for comp in range(6):
        into = f.at[comp, pl.ds(first, 8), pl.ds(8, ROWS), :]
        copies.append(pltpu.make_async_copy(t_hbm.at[comp], into, sems.at[comp]))
    copies.append(pltpu.make_async_copy(t_hbm.at[6], coef.at[pl.ds(first, 8)], sems.at[6]))
    copies.append(pltpu.make_async_copy(below_hbm, halo.at[0], sems.at[7]))
    copies.append(pltpu.make_async_copy(above_hbm, halo.at[1], sems.at[8]))
    return copies


def merge(f, coef, halo, first, col, last):
    low = lanes() < 64
    for comp in range(7):
        for x in range(8):
            below, above = halo[0, comp, x % 4], halo[1, comp, x % 4]
            below = jnp.where(col > 0, swap(below) if x >= 4 else below, 0.0)
            above = jnp.where(col < last, swap(above) if x < 4 else above, 0.0)
            if comp < 6:
                f[comp, first + x, tile(0)] = jnp.where(low, below, f[comp, first + x, tile(0)])
                f[comp, first + x, tile(TILES - 1)] = jnp.where(low, f[comp, first + x, tile(TILES - 1)], above)
            else:
                coef[first + x, 0:8] = jnp.where(low, below, coef[first + x, 0:8])
                coef[first + x, ROWS - 8 : ROWS] = jnp.where(low, coef[first + x, ROWS - 8 : ROWS], above)


def absorber(positions, total, low, high):
    depth = jnp.maximum(
        jnp.maximum((low - positions) / low, (positions - (total - 1.0 - high)) / high), 0.0
    )
    sigma = sigma_top * depth**3
    damp = jnp.exp(-(sigma + alpha_shift) * time_step)
    gain = sigma / (sigma + alpha_shift) * (damp - 1.0)
    return (damp, gain)


def tables(sc_ref, xt_ref, yt_ref, hc_ref, planes, full_x, full_y):
    widths = [sc_ref[i].astype(jnp.float32) for i in range(4)]
    row, col = sc_ref[4], sc_ref[5]
    for p, x in planes:
        at = jnp.full((8, 128), (row * 8 + x).astype(jnp.float32))
        for k, shift in ((0, 0.5), (2, 0.0)):
            damp, gain = absorber(at + shift, float(full_x), widths[0], widths[1])
            xt_ref[k, p] = damp
            xt_ref[k + 1, p] = gain
    for t in range(TILES):
        half = jnp.where(lanes() < 64, 0, 64)
        y = col * 128 + half + 8 * t - STEPS + lax.broadcasted_iota(jnp.int32, (8, 128), 0)
        at = y.astype(jnp.float32)
        for k, shift in ((0, 0.5), (2, 0.0)):
            damp, gain = absorber(at + shift, float(full_y), widths[2], widths[3])
            yt_ref[k, 8 * t : 8 * t + 8] = damp
            yt_ref[k + 1, 8 * t : 8 * t + 8] = gain
        step = jnp.where(y >= 0, time_step, 0.0)
        hc_ref[0, 8 * t : 8 * t + 8] = step
        hc_ref[1, 8 * t : 8 * t + 8] = jnp.where(row > 0, step, 0.0)


def magnetic(f, psi, p, xt, yt, hc, which):
    z_last = (lanes() & 63) == 63
    damp_x, gain_x = xt[0, p], xt[1, p]
    for t in range(TILES):
        here, rows = tile(t), slice(8 * t, 8 * t + 8)
        e_x, e_y, e_z = f[0, p, here], f[1, p, here], f[2, p, here]
        ez_dy = f[2, p, tile(t, 1)] - e_z
        ex_dy = f[0, p, tile(t, 1)] - e_x
        ey_dz = jnp.where(z_last, 0.0, pltpu.roll(e_y, 127, 1)) - e_y
        ex_dz = jnp.where(z_last, 0.0, pltpu.roll(e_x, 127, 1)) - e_x
        ez_dx = f[2, p + 1, here] - e_z
        ey_dx = f[1, p + 1, here] - e_y
        damp_y, gain_y, step = yt[0, rows], yt[1, rows], hc[which, rows]
        psi_hxy = damp_y * psi[0, p, rows] + gain_y * ez_dy
        psi_hyx = damp_x * psi[1, p, rows] + gain_x * ez_dx
        psi_hzx = damp_x * psi[2, p, rows] + gain_x * ey_dx
        psi_hzy = damp_y * psi[3, p, rows] + gain_y * ex_dy
        psi[0, p, rows] = psi_hxy
        psi[1, p, rows] = psi_hyx
        psi[2, p, rows] = psi_hzx
        psi[3, p, rows] = psi_hzy
        f[3, p, here] = f[3, p, here] - step * (ez_dy + psi_hxy - ey_dz)
        f[4, p, here] = f[4, p, here] - step * (ex_dz - ez_dx - psi_hyx)
        f[5, p, here] = f[5, p, here] - step * (ey_dx + psi_hzx - ex_dy - psi_hzy)


def electric(f, psi, coef, p, xt, yt):
    z_first = (lanes() & 63) == 0
    damp_x, gain_x = xt[2, p], xt[3, p]
    for t in range(TILES):
        here, rows = tile(t), slice(8 * t, 8 * t + 8)
        h_x, h_y, h_z = f[3, p, here], f[4, p, here], f[5, p, here]
        hz_dy = h_z - f[5, p, tile(t, -1)]
        hx_dy = h_x - f[3, p, tile(t, -1)]
        hy_dz = h_y - jnp.where(z_first, 0.0, pltpu.roll(h_y, 1, 1))
        hx_dz = h_x - jnp.where(z_first, 0.0, pltpu.roll(h_x, 1, 1))
        hz_dx = h_z - f[5, p - 1, here]
        hy_dx = h_y - f[4, p - 1, here]
        damp_y, gain_y, step = yt[2, rows], yt[3, rows], coef[p, rows]
        psi_exy = damp_y * psi[4, p, rows] + gain_y * hz_dy
        psi_eyx = damp_x * psi[5, p, rows] + gain_x * hz_dx
        psi_ezx = damp_x * psi[6, p, rows] + gain_x * hy_dx
        psi_ezy = damp_y * psi[7, p, rows] + gain_y * hx_dy
        psi[4, p, rows] = psi_exy
        psi[5, p, rows] = psi_eyx
        psi[6, p, rows] = psi_ezx
        psi[7, p, rows] = psi_ezy
        f[0, p, here] = f[0, p, here] + step * (hz_dy + psi_exy - hy_dz)
        f[1, p, here] = f[1, p, here] + step * (hx_dz - hz_dx - psi_eyx)
        f[2, p, here] = f[2, p, here] + step * (hy_dx + psi_ezx - hx_dy - psi_ezy)


def pack(read, out_ref, at):
    low = lanes() < 64
    for t in range(TILES - 1):
        out_ref[pl.ds(pl.multiple_of(at * SENT + 8 * t, 8), 8), :] = jnp.where(low, read(t), read(t + 1))


def unpack(ref, at, t):
    low = lanes() < 64

    def get(k):
        return ref[pl.ds(pl.multiple_of(at * SENT + 8 * k, 8), 8), :]

    first = get(t) if t < TILES - 1 else swap(get(0))
    second = get(t - 1) if t > 0 else swap(get(TILES - 2))
    return jnp.where(low, first, second)


def zero_planes(ref, comps, planes, rows):
    zero = jnp.zeros((rows, 128), jnp.float32)

    def one(p, carry):
        for c in comps:
            ref[c, p] = zero
        return carry

    lax.fori_loop(planes[0], planes[1], one, 0)


def zero_edges(f, first):
    zero = jnp.zeros((8, 128), jnp.float32)
    for comp in range(6):
        for x in range(8):
            f[comp, first + x, 0:8] = zero
            f[comp, first + x, ROWS + 8 : ROWS + 16] = zero


def groups(number, body):
    for i in range(2):
        if isinstance(number, int):
            body(i)
        else:
            pl.when(i < number)(functools.partial(body, i))


def alone(full_x, full_y, last, begin, end, sc, t_hbm, below_hbm, above_hbm, *rest):
    up_ref, down_ref, f, psi, coef, xt, yt, hc, halo, sems = rest
    col = sc[5]
    copies = fill(f, coef, t_hbm, below_hbm, above_hbm, halo, sems, 1)
    for copy in copies:
        copy.start()
    tables(sc, xt, yt, hc, [(1 + x, x) for x in range(8)], full_x, full_y)
    zero_planes(psi, range(8), (1, 9), ROWS)
    zero_planes(f, range(6), (0, 1), ROWS + 16)
    zero_planes(f, range(6), (9, 10), ROWS + 16)
    zero_edges(f, 1)
    for copy in copies:
        copy.wait()
    merge(f, coef, halo, 1, col, last)
    if begin == 0:
        low = lanes() < 64
        for k in range(DEEP):
            at = 2 * end * SENT + 8 * k
            up_ref[at : at + 8] = jnp.where(low, coef[5 + k, 0:8], coef[5 + k, ROWS - 8 : ROWS])
            down_ref[at : at + 8] = jnp.where(low, coef[1 + k, 0:8], coef[1 + k, ROWS - 8 : ROWS])

    def step(s, carry):
        @pl.when(s >= begin)
        def _():
            for c in range(2):
                pack(lambda t: f[1 + c, 1, tile(t)], down_ref, 2 * (s - begin) + c)

        def h_four(i):
            for x in (2 * i, 2 * i + 1, 7 - 2 * i, 6 - 2 * i):
                magnetic(f, psi, 1 + x, xt, yt, hc, 0)

        def e_four(i):
            for x in (2 * i, 2 * i + 1, 7 - 2 * i, 6 - 2 * i):
                electric(f, psi, coef, 1 + x, xt, yt)

        reach = jnp.minimum(4, end - s)
        groups((reach + 1) // 2, h_four)

        @pl.when(s >= begin)
        def _():
            for c in range(2):
                pack(lambda t: f[4 + c, 8, tile(t)], up_ref, 2 * (s - begin) + c)

        reach = jnp.minimum(4, end - 1 - s)
        groups((reach + 1) // 2, e_four)
        return carry

    lax.fori_loop(0, end, step, 0)


CELLS = [(1 + k, k - 4) for k in range(4)] + [(6 + x, x) for x in range(8)] + [(15 + k, 8 + k) for k in range(4)]


def before_magnetic(f, came):
    for c in range(2):
        for t in range(TILES):
            here = tile(t)
            f[1 + c, 14, here] = f[1 + c, 15, here] + came(c, t)
            f[1 + c, 5, here] = f[1 + c, 6, here]


def before_electric(f, came):
    for c in range(2):
        for t in range(TILES):
            here = tile(t)
            f[4 + c, 5, here] = f[4 + c, 4, here] + came(c, t)
            f[4 + c, 14, here] = f[4 + c, 13, here]


def h_side(f, psi, xt, yt, hc):
    def body(i):
        for k in (2 * i, 2 * i + 1):
            magnetic(f, psi, 4 - k, xt, yt, hc, 1)
            magnetic(f, psi, 15 + k, xt, yt, hc, 0)

    return body


def e_side(f, psi, coef, xt, yt):
    def body(i):
        for k in (2 * i, 2 * i + 1):
            electric(f, psi, coef, 4 - k, xt, yt)
            electric(f, psi, coef, 15 + k, xt, yt)

    return body


def h_own(f, psi, xt, yt, hc):
    def body(i):
        for x in (2 * i, 2 * i + 1, 7 - 2 * i, 6 - 2 * i):
            magnetic(f, psi, 6 + x, xt, yt, hc, 0)

    return body


def e_own(f, psi, coef, xt, yt):
    def body(i):
        for x in (2 * i, 2 * i + 1, 7 - 2 * i, 6 - 2 * i):
            electric(f, psi, coef, 6 + x, xt, yt)

    return body


def joined(
    full_x, full_y, last_row, last, early, sc, t_hbm, below_hbm, above_hbm, left_ref, right_ref, cleft_ref,
    cright_ref, end_hbm, f, psi, coef, xt, yt, hc, halo, sems,
):
    row, col = sc[4], sc[5]
    copies = fill(f, coef, t_hbm, below_hbm, above_hbm, halo, sems, 6)
    for copy in copies:
        copy.start()
    tables(sc, xt, yt, hc, CELLS, full_x, full_y)
    zero_planes(psi, range(8), (1, 19), ROWS)
    zero_planes(f, range(6), (0, 6), ROWS + 16)
    zero_planes(f, range(6), (14, 20), ROWS + 16)
    zero_edges(f, 6)
    for copy in copies:
        copy.wait()
    merge(f, coef, halo, 6, col, last)
    low = lanes() < 64
    for ref, edge_ref, first, there in (
        (cleft_ref, left_ref, 1, row > 0),
        (cright_ref, right_ref, 15, row < last_row),
    ):
        for k in range(DEEP):
            at = 2 * early * SENT + 8 * k
            corner = edge_ref[at : at + 8]
            for t in range(TILES):
                if t == 0:
                    value = jnp.where(low, corner, swap(ref[k, HALF - 8 : HALF]))
                elif t == TILES - 1:
                    value = jnp.where(low, swap(ref[k, 0:8]), corner)
                else:
                    value = ref[k, 8 * t - 8 : 8 * t]
                coef[first + k, 8 * t : 8 * t + 8] = jnp.where(there, value, 0.0)

    out = pltpu.make_async_copy(coef, end_hbm.at[pl.ds(48, 20)], sems.at[6])
    out.start()

    def step(s, carry):
        deep = jnp.minimum(s + 1, STEPS - s)
        at = 2 * jnp.minimum(s, early - 1)
        from_above = jnp.logical_and(row < last_row, s < early)
        from_below = jnp.logical_and(row > 0, s < early)
        before_magnetic(f, lambda c, t: jnp.where(from_above, unpack(right_ref, at + c, t), 0.0))
        groups(2, h_own(f, psi, xt, yt, hc))
        groups((deep + 1) // 2, h_side(f, psi, xt, yt, hc))
        before_electric(f, lambda c, t: jnp.where(from_below, unpack(left_ref, at + c, t), 0.0))
        groups(2, e_own(f, psi, coef, xt, yt))
        groups((deep + 1) // 2, e_side(f, psi, coef, xt, yt))
        return carry

    lax.fori_loop(0, STEPS, step, 0)
    out.wait()
    outs = []
    for comp in range(6):
        own = f.at[comp, pl.ds(6, 8), pl.ds(8, ROWS), :]
        outs.append(pltpu.make_async_copy(own, end_hbm.at[pl.ds(8 * comp, 8)], sems.at[comp]))
        outs[comp].start()
    for copy in outs:
        copy.wait()


def late(
    full_x, full_y, last_row, early, count, sc, snap, end_hbm, left_ref, right_ref, modes_hbm,
    out_ref, e_out, h_out, f, psi, coef, xt, yt, hc, end_ref, modes_ref, planes, snaps, gram_ref, sems,
):
    row = sc[4]
    coef_in = pltpu.make_async_copy(end_hbm.at[pl.ds(48, 20)], coef, sems.at[2])
    end_in = pltpu.make_async_copy(end_hbm.at[pl.ds(0, 48)], end_ref, sems.at[3])
    modes_in = pltpu.make_async_copy(modes_hbm, modes_ref, sems.at[4])
    for copy in (coef_in, end_in, modes_in):
        copy.start()
    tables(sc, xt, yt, hc, CELLS, full_x, full_y)
    zero_planes(f, range(6), (2, 18), ROWS + 16)
    zero_planes(psi, range(8), (3, 17), ROWS)
    coef_in.wait()
    count_late = STEPS - early

    def step(j, carry):
        deep = jnp.minimum(j + 1, count_late - j)
        reach = jnp.minimum(j + 1, 4)
        before_magnetic(f, lambda c, t: jnp.where(row < last_row, unpack(right_ref, 2 * j + c, t), 0.0))
        groups((reach + 1) // 2, h_own(f, psi, xt, yt, hc))
        groups((deep + 1) // 2, h_side(f, psi, xt, yt, hc))
        before_electric(f, lambda c, t: jnp.where(row > 0, unpack(left_ref, 2 * j + c, t), 0.0))
        groups((reach + 1) // 2, e_own(f, psi, coef, xt, yt))
        groups((deep + 1) // 2, e_side(f, psi, coef, xt, yt))
        return carry

    lax.fori_loop(0, count_late, step, 0)
    end_in.wait()

    low = lax.broadcasted_iota(jnp.int32, (HALF, 128), 1) < 64
    own = slice(8 + STEPS, 8 + STEPS + HALF)
    for comp in range(6):
        for j in range(4):
            first = f[comp, 6 + j, own] + end_ref[8 * comp + j, STEPS : STEPS + HALF]
            second = f[comp, 10 + j, own] + end_ref[8 * comp + 4 + j, STEPS : STEPS + HALF]
            top = jnp.where(low, first, swap(second))
            bottom = jnp.where(low, swap(first), second)
            turned = jnp.concatenate([top, bottom], 0).T
            planes[pl.ds(comp * 8 * NZ + j, NZ, stride=8), :] = turned[:NZ]
            planes[pl.ds(comp * 8 * NZ + j + 4, NZ, stride=8), :] = turned[NZ:]
    size = 3 * NZ * 8
    copies = [
        pltpu.make_async_copy(planes.at[pl.ds(0, size)], e_out, sems.at[0]),
        pltpu.make_async_copy(planes.at[pl.ds(size, size)], h_out, sems.at[1]),
    ]
    for copy in copies:
        copy.start()
    modes_in.wait()
    for s in range(count):
        snaps[8 * s : 8 * s + 8] = planes[pl.ds(pl.multiple_of(snap[s] * 8, 8), 8), :]
    gram = jnp.zeros((count, count), jnp.float32)
    coefficients = jnp.zeros((count, 128), jnp.float32)
    contract = functools.partial(
        lax.dot_general,
        dimension_numbers=(((1,), (1,)), ((), ())),
        precision=lax.Precision.HIGHEST,
        preferred_element_type=jnp.float32,
    )
    for x in range(8):
        part = snaps[pl.ds(x, count, stride=8), :]
        gram = gram + contract(part, part)
        coefficients = coefficients + contract(part, modes_ref[pl.ds(x, 128, stride=8), :])
    gram_ref[...] = jnp.concatenate([gram[:32], gram[32:]], 1) / float(full_x * full_y)
    for b in range(8):
        out_ref[b, 0:8] = coefficients[8 * b : 8 * b + 8]
        out_ref[b, 8:12] = gram_ref[4 * b : 4 * b + 4]
    for copy in copies:
        copy.wait()


def around(block, axis, distance):
    size = lax.axis_size(axis)
    return lax.ppermute(block, axis, [(i, (i + distance) % size) for i in range(size)])


def spread(block, axes, size):
    whole = jnp.broadcast_to(block, (size,) + block.shape)
    return lax.all_to_all(whole, axes, split_axis=0, concat_axis=0, tiled=True)


def f32(*shape):
    return jax.ShapeDtypeStruct(shape, jnp.float32)


def call(kernel, flops, limit, **kwargs):
    return pl.pallas_call(
        kernel,
        compiler_params=pltpu.CompilerParams(vmem_limit_bytes=limit * 1024 * 1024),
        cost_estimate=pl.CostEstimate(flops=flops, bytes_accessed=4_000_000, transcendentals=0),
        **kwargs,
    )


def scratch(planes, *more):
    shapes = [(6, planes, ROWS + 16, 128), (8, planes, ROWS, 128), (planes, ROWS, 128)]
    shapes = shapes + [(4, planes, 8, 128), (4, ROWS, 128), (2, ROWS, 128)] + list(more)
    return [pltpu.VMEM(shape, jnp.float32) for shape in shapes]


HALO = (2, 7, 4, 8, 128)
EARLY = 4


def shards(e_field, h_field, e_coef, basis, pml_width, snap_index):
    rows_count, cols_count = lax.axis_size(ROW), lax.axis_size(COL)
    full_x, full_y = 8 * rows_count, 128 * cols_count
    row, col = lax.axis_index(ROW), lax.axis_index(COL)
    count = snap_index.shape[0]
    scalars = jnp.concatenate([pml_width, jnp.stack([row, col]).astype(jnp.int32)])
    vmem = pl.BlockSpec(memory_space=pltpu.VMEM)
    smem = pl.BlockSpec(memory_space=pltpu.SMEM)
    hbm = pl.BlockSpec(memory_space=pltpu.HBM)

    turned, up, down, c_up, c_down = call(
        prepare, 10**9, PREPARE_MIB,
        out_shape=(f32(7, 8, ROWS, 128),) + (f32(7, 4, 8, 128),) * 2 + (f32(4, HALF, 128),) * 2,
        in_specs=[hbm] * 3,
        out_specs=(hbm,) + (vmem,) * 4,
        scratch_shapes=[
            pltpu.VMEM((7, 512, 128), jnp.float32),
            pltpu.VMEM((7, 8, ROWS, 128), jnp.float32),
            pltpu.SemaphoreType.DMA((14,)),
        ],
    )(e_field.reshape(3, 512, 128), h_field.reshape(3, 512, 128), e_coef.reshape(1, 512, 128))
    below, above = around(up, COL, 1), around(down, COL, -1)
    c_left, c_right = around(c_up, ROW, 1), around(c_down, ROW, -1)

    def run_alone(begin, end):
        sent = f32(2 * (end - begin) * SENT + (8 * DEEP if begin == 0 else 0), 128)
        return call(
            functools.partial(alone, full_x, full_y, cols_count - 1, begin, end), 4 * 10**9, ALONE_MIB,
            out_shape=(sent, sent),
            in_specs=[smem] + [hbm] * 3,
            out_specs=(vmem,) * 2,
            scratch_shapes=scratch(10, HALO) + [pltpu.SemaphoreType.DMA((9,))],
        )(scalars, turned, below, above)

    with jax.named_scope("alone_a"):
        up, down = run_alone(0, EARLY)
    left, right = around(up, ROW, 1), around(down, ROW, -1)
    with jax.named_scope("alone_b"):
        up, down = run_alone(EARLY, STEPS)
    with jax.named_scope("turn"):
        modes, up = lax.optimization_barrier((basis, up))
        modes = modes.reshape(16, rows_count, 8, 128).transpose(1, 0, 2, 3)
        modes = lax.all_to_all(modes, ROW, split_axis=0, concat_axis=0, tiled=True).reshape(1024, 128)
    up, down, left, right = lax.optimization_barrier((up, down, left, right))
    left_late, right_late = around(up, ROW, 1), around(down, ROW, -1)

    with jax.named_scope("joined"):
        ends = call(
            functools.partial(joined, full_x, full_y, rows_count - 1, cols_count - 1, EARLY), 12 * 10**9, JOINED_MIB,
            out_shape=f32(68, ROWS, 128),
            in_specs=[smem] + [hbm] * 3 + [vmem] * 4,
            out_specs=hbm,
            scratch_shapes=scratch(20, HALO) + [pltpu.SemaphoreType.DMA((9,))],
        )(scalars, turned, below, above, left, right, c_left, c_right)

    sums, e_final, h_final = call(
        functools.partial(late, full_x, full_y, rows_count - 1, EARLY, count), 4 * 10**9, LATE_MIB,
        out_shape=(f32(8, 12, 128), f32(1536, 128), f32(1536, 128)),
        in_specs=[smem] * 2 + [hbm] + [vmem] * 2 + [hbm],
        out_specs=(vmem, hbm, hbm),
        scratch_shapes=scratch(20, (48, ROWS, 128), (1024, 128))
        + [
            pltpu.VMEM((6 * NZ * 8, 128), jnp.float32),
            pltpu.VMEM((count * 8, 128), jnp.float32),
            pltpu.VMEM((32, 128), jnp.float32),
            pltpu.SemaphoreType.DMA((5,)),
        ],
    )(scalars, snap_index, ends, left_late, right_late, modes)

    part = lax.all_to_all(sums, NEAR, split_axis=0, concat_axis=0, tiled=True).sum(0)
    part = spread(part, FAR, lax.axis_size(FAR)).sum(0)
    whole = spread(part, NEAR, lax.axis_size(NEAR))
    coefficients = whole[:, :8].reshape(count, 128)
    packed = whole[:, 8:].reshape(count // 2, 128)
    gram = jnp.concatenate([packed[:, :64], packed[:, 64:]], 0)
    shape = e_field.shape
    return (e_final.reshape(shape), h_final.reshape(shape), coefficients, gram)


PREPARE_MIB, ALONE_MIB, JOINED_MIB, LATE_MIB = 56, 60, 60, 60


def solution(mesh):
    split = Mesh(mesh.devices.reshape(4, 2, 8, 2, 2), ROW + COL)
    return jax.shard_map(
        shards,
        mesh=split,
        in_specs=(
            P(None, None, ROW, COL),
            P(None, None, ROW, COL),
            P(None, ROW, COL),
            P(ROW, None, COL),
            P(),
            P(),
        ),
        out_specs=(P(None, None, ROW, COL), P(None, None, ROW, COL), P(), P()),
        check_vma=False,
    )
```

time: 135 us -> 118 us (0.87)
  blocking collectives: 78.4 us -> 43.2 us
  starting transfers between devices: 8.28 us -> 22.4 us
  Pallas kernels: 39.1 us -> 44.7 us
  waiting for transfers between devices: 2.69 us -> 0.42 us
    all_to_all x1 -> x0, blocking collectives: 38.3 us -> none  [shards(): lax.all_to_all(basis, ROW, split_axis=1, concat_axis=0, tiled=True)]
    ppermute x4 -> x8, starting transfers between devices: 8.28 us -> 19 us  [around(): lax.ppermute(block, axis, [(i, (i + distance) % size) for i in range(size)])]
    all_to_all x1, blocking collectives: 8.6 us -> 14.2 us  [shards(): lax.all_to_all(sums, NEAR, split_axis=0, concat_axis=0, tiled=True).sum(0)]
    pallas_call x3 -> x5, Pallas kernels: 39.1 us -> 44.7 us  [the longest x1 15.8 us: shards(): call(functools.partial(joined, full_x, full_y, rows_count - 1, cols_count...]
    all_to_all x0 -> x1, starting transfers between devices: none -> 3.49 us  [shards(): lax.all_to_all(modes, ROW, split_axis=0, concat_axis=0, tiled=True)]
    all_to_all x2, blocking collectives: 31.5 us -> 28.9 us  [spread(): return lax.all_to_all(whole, axes, split_axis=0, concat_axis=0, tiled=True)]
    ppermute x4 -> x8, waiting for transfers between devices: 2.69 us -> 0.42 us  [around(): lax.ppermute(block, axis, [(i, (i + distance) % size) for i in range(size)])]
  transfers between devices with their start and end apart: 4 -> 9, of which waited for: 2 -> 1; matrix products, arithmetic and copies ran while one was open for 2% -> 1% of each run, Pallas kernels for 0% -> 26%
where the time goes in v2:
time: 118 us; the launch traced here: 117 us
  Pallas kernels  44.7 us (38%)
  blocking collectives  43.2 us (37%)
  starting transfers between devices  22.4 us (19%)
  local copies, waits for them, and re-layouts  4.25 us (4%)
  other arithmetic  1.34 us (1%)
    all_to_all x2, blocking collectives, spread(): return lax.all_to_all(whole, axes, split_axis=0, concat_axis=0, tiled=True)  28.9 us
    ppermute x8, starting transfers between devices, around(): lax.ppermute(block, axis, [(i, (i + distance) % size) for i in range(size)])  19 us
    pallas_call x1, Pallas kernels, shards(): call(functools.partial(joined, full_x, full_y, rows_count - 1, cols_count...  15.8 us
    pallas_call x2, Pallas kernels, run_alone(): call(functools.partial(alone, full_x, full_y, cols_count - 1, begin, end)...  14.4 us
    all_to_all x1, blocking collectives, shards(): lax.all_to_all(sums, NEAR, split_axis=0, concat_axis=0, tiled=True).sum(0)  14.2 us
    pallas_call x1, Pallas kernels, shards(): call(functools.partial(late, full_x, full_y, rows_count - 1, EARLY, count...  10 us
    pallas_call x1, Pallas kernels, shards(): call(prepare, 10 ** 9, PREPARE_MIB, out_shape=(f32(7, 8, ROWS, 128),) + (...  4.47 us
    all_to_all x1, starting transfers between devices, shards(): lax.all_to_all(modes, ROW, split_axis=0, concat_axis=0, tiled=True)  3.49 us
  transfers between devices with their start and end apart: 9, of which 1 were waited for; matrix products, arithmetic and copies ran while one was open for 1% of the time, Pallas kernels for 26%

profile of v2, /device:TPU:1, one launch (start us, length us, event | category | flops | bytes accessed | tf_op | source)
XLA Modules:
  0.0 117.2 jit_solution(12942323868051994736)
XLA Ops:
  0.6 0.0 copy-start
  0.7 4.5 %shard_map.93 = (f32[7,8,80,128]{3,2,1,0:T(8,128)}, f32[7,4,8,128]{3,2,1,0:T(8,128)}, f32[7,4,8,128]{3,2,1,0:T(8,128)}, f32[4,64,128]{2,1,0:T(8,128)}, f32[4,64,128]{2,1,0:T(8,128)}) custom-call(f32[3,512,128]{2,1,0:T(8,128)} %bitcast.18, f32[3,512,128]{2,1,0:T(8,128)} %bitcast.19, f32[1,512,128]{2,1,0:T(8,128)} %bitcast.20), custom_call_target="tpu_custom_call" | custom-call | flops 1000000000 | bytes 4000000 | tf_op jit(solution)/shard_map/pallas_call | solution.py:508
  5.1 2.8 %collective-permute-start = (f32[7,4,8,128]{3,2,1,0:T(8,128)}, f32[7,4,8,128]{3,2,1,0:T(8,128)S(1)}, u32[]{:S(2)}, u32[]{:S(2)}) collective-permute-start(f32[7,4,8,128]{3,2,1,0:T(8,128)} %get-tuple-element.23), channel_id=1, source_target_pairs={{0,1},{1,2},{2,3},{3,4},{4,5},{5,6},{6,7},{7,8},{8,9},{9,10},{10,1... | collective-permute-start | bytes 344072 | tf_op jit(solution)/shard_map/ppermute | solution.py:467
  7.9 0.6 collective-permute-start.1
  8.5 2.0 %collective-permute-start.4 = (f32[4,64,128]{2,1,0:T(8,128)}, f32[4,64,128]{2,1,0:T(8,128)S(1)}, u32[]{:S(2)}, u32[]{:S(2)}) collective-permute-start(f32[4,64,128]{2,1,0:T(8,128)} %get-tuple-element.32), channel_id=1, source_target_pairs={{0,32},{32,64},{64,96},{96,128},{128,160},{160,192},{192,224},{224... | collective-permute-start | bytes 393224 | tf_op jit(solution)/shard_map/ppermute | solution.py:467
  10.5 3.1 %collective-permute-start.5 = (f32[4,64,128]{2,1,0:T(8,128)}, f32[4,64,128]{2,1,0:T(8,128)S(1)}, u32[]{:S(2)}, u32[]{:S(2)}) collective-permute-start(f32[4,64,128]{2,1,0:T(8,128)} %get-tuple-element.33), channel_id=1, source_target_pairs={{0,224},{32,0},{64,32},{96,64},{128,96},{160,128},{192,160},{224,1... | collective-permute-start | bytes 393224 | tf_op jit(solution)/shard_map/ppermute | solution.py:467
  13.6 0.7 pad_add_fusion.sc
  14.3 0.6 copy-done.9
  14.9 0.0 copy-done.10
  15.0 5.5 %alone_a.1 = (f32[608,128]{1,0:T(8,128)}, f32[608,128]{1,0:T(8,128)}) custom-call(s32[6]{0:T(128)} %pad_add_fusion.sc, f32[7,8,80,128]{3,2,1,0:T(8,128)} %get-tuple-element.22.t_hbm, f32[7,4,8,128]{3,2,1,0:T(8,128)} %copy-done.9, f32[7,4,8,128]{3,2,1,0:T(8,128)} %copy-done.10), custom_call_target="tpu_custom_call" | custom-call | flops 4000000000 | bytes 4000000 | tf_op jit(solution)/shard_map/alone_a/pallas_call | solution.py:524
  20.5 0.7 collective-permute-start.2
  21.2 4.5 %collective-permute-start.3 = (f32[608,128]{1,0:T(8,128)}, f32[608,128]{1,0:T(8,128)S(1)}, u32[]{:S(2)}, u32[]{:S(2)}) collective-permute-start(f32[608,128]{1,0:T(8,128)} %get-tuple-element.29), channel_id=1, source_target_pairs={{0,224},{32,0},{64,32},{96,64},{128,96},{160,128},{192,160},{224,1... | collective-permute-start | bytes 933896 | tf_op jit(solution)/shard_map/ppermute | solution.py:467
  25.6 8.9 %alone_b.1 = (f32[576,128]{1,0:T(8,128)}, f32[576,128]{1,0:T(8,128)}) custom-call(s32[6]{0:T(128)} %pad_add_fusion.sc, f32[7,8,80,128]{3,2,1,0:T(8,128)} %get-tuple-element.22.t_hbm, f32[7,4,8,128]{3,2,1,0:T(8,128)} %copy-done.9, f32[7,4,8,128]{3,2,1,0:T(8,128)} %copy-done.10), custom_call_target="tpu_custom_call" | custom-call | flops 4000000000 | bytes 4000000 | tf_op jit(solution)/shard_map/alone_b/pallas_call | solution.py:524
  34.6 0.8 copy_bitcast_fusion
  35.4 3.5 %all-to-all-start = ((f32[8,16,8,128]{3,2,1,0:T(8,128)}), f32[8,16,8,128]{3,2,1,0:T(8,128)S(1)}, u32[]{:S(2)}, u32[]{:S(2)}) async-start(f32[8,16,8,128]{3,2,1,0:T(8,128)} %copy_bitcast_fusion), calls=%async_computation | async-start | bytes 1048576 | tf_op jit(solution)/shard_map/turn/all_to_all | solution.py:540
  38.9 0.0 copy-start.3
  38.9 2.9 %collective-permute-start.6 = (f32[576,128]{1,0:T(8,128)}, f32[576,128]{1,0:T(8,128)S(1)}, u32[]{:S(2)}, u32[]{:S(2)}) collective-permute-start(f32[576,128]{1,0:T(8,128)} %get-tuple-element.34), channel_id=1, source_target_pairs={{0,32},{32,64},{64,96},{96,128},{128,160},{160,192},{192,224},{224... | collective-permute-start | bytes 884744 | tf_op jit(solution)/shard_map/ppermute | solution.py:467
  41.9 2.4 %collective-permute-start.7 = (f32[576,128]{1,0:T(8,128)}, f32[576,128]{1,0:T(8,128)S(1)}, u32[]{:S(2)}, u32[]{:S(2)}) collective-permute-start(f32[576,128]{1,0:T(8,128)} %get-tuple-element.35), channel_id=1, source_target_pairs={{0,224},{32,0},{64,32},{96,64},{128,96},{160,128},{192,160},{224,1... | collective-permute-start | bytes 884744 | tf_op jit(solution)/shard_map/ppermute | solution.py:467
  44.3 0.6 copy-done.7
  44.9 0.7 copy-done.8
  45.6 15.8 %joined.1.end_hbm = f32[68,80,128]{2,1,0:T(8,128)} custom-call(s32[6]{0:T(128)} %pad_add_fusion.sc, f32[7,8,80,128]{3,2,1,0:T(8,128)} %get-tuple-element.22.t_hbm, f32[7,4,8,128]{3,2,1,0:T(8,128)} %copy-done.9, f32[7,4,8,128]{3,2,1,0:T(8,128)} %copy-done.10, f32[608,128]{1,0:T(8,128)} %copy-done.3, f32[608,128]{1,0:T(8,128)} %copy-done.4, ...), custom_call_target="tpu_custom_call" | custom-call | flops 12000000000 | bytes 4000000 | tf_op jit(solution)/shard_map/joined/pallas_call | solution.py:545
  61.4 0.4 collective-permute-done.7.right_ref
  61.8 0.4 copy-done.1
  62.2 0.1 copy-done.5
  62.3 0.2 copy-done.6
  62.6 10.0 %shard_map.94 = (f32[8,12,128]{2,1,0:T(8,128)}, f32[1536,128]{1,0:T(8,128)}, f32[1536,128]{1,0:T(8,128)}) custom-call(s32[6]{0:T(128)} %pad_add_fusion.sc, s32[64]{0:T(128)} %snap.1, f32[68,80,128]{2,1,0:T(8,128)} %joined.1.end_hbm, f32[576,128]{1,0:T(8,128)} %copy-done.5, f32[576,128]{1,0:T(8,128)} %copy-done.6, f32[1024,128]{1,0:T(8,128)} %bitcast.16), custom_call_target="tpu_custom_call" | custom-call | flops 4000000000 | bytes 4000000 | tf_op jit(solution)/shard_map/pallas_call | solution.py:553
  72.6 14.2 %all_to_all.20 = f32[8,12,128]{2,1,0:T(8,128)S(1)} all-to-all(f32[8,12,128]{2,1,0:T(8,128)} %get-tuple-element.39), channel_id=1, replica_groups=mesh['row_0'=4,'row_1'=2,'col_0'=8,'col_1'=2,'col_2'=2] {'row_1','col_1'..., dimensions={0} | all-to-all | bytes 98304 | tf_op jit(solution)/shard_map/all_to_all | solution.py:567
  86.9 18.0 %all_to_all.21 = f32[32,12,128]{2,1,0:T(8,128)S(1)} all-to-all(f32[32,12,128]{2,1,0:T(8,128)S(1)} %broadcast_in_dim.6), channel_id=1, replica_groups=mesh['row_0'=4,'row_1'=2,'col_0'=8,'col_1'=2,'col_2'=2] {'row_0','col_0'}, dimensions={0} | all-to-all | bytes 393216 | tf_op jit(solution)/shard_map/all_to_all | solution.py:472
  104.9 11.0 %all_to_all.22 = f32[8,12,128]{2,1,0:T(8,128)S(1)} all-to-all(f32[8,12,128]{2,1,0:T(8,128)S(1)} %broadcast_in_dim.7), channel_id=1, replica_groups=mesh['row_0'=4,'row_1'=2,'col_0'=8,'col_1'=2,'col_2'=2] {'row_1','col_1'..., dimensions={0} | all-to-all | bytes 98304 | tf_op jit(solution)/shard_map/all_to_all | solution.py:472
  115.8 0.1 fusion
  115.9 0.6 pad_maximum_fusion
  116.5 0.6 slice_bitcast_fusion
  (26 shorter events, 0.1 us)
Async XLA Ops:
  0.6 33.9 %copy-start = (f32[16,64,128]{2,1,0:T(8,128)S(1)}, f32[16,64,128]{2,1,0:T(8,128)}, u32[]{:S(2)}) copy-start(f32[16,64,128]{2,1,0:T(8,128)} %param.9) | copy-start | bytes 1572868
  0.6 12.9 %copy-start.2 = (s32[4]{0:T(128)S(1)}, s32[4]{0:T(128)}, u32[]{:S(2)}) copy-start(s32[4]{0:T(128)} %param.10) | copy-start | bytes 52
  5.1 9.1 %collective-permute-start = (f32[7,4,8,128]{3,2,1,0:T(8,128)}, f32[7,4,8,128]{3,2,1,0:T(8,128)S(1)}, u32[]{:S(2)}, u32[]{:S(2)}) collective-permute-start(f32[7,4,8,128]{3,2,1,0:T(8,128)} %get-tuple-element.23), channel_id=1, source_target_pairs={{0,1},{1,2},{2,3},{3,4},{4,5},{5,6},{6,7},{7,8},{8,9},{9,10},{10,1... | collective-permute-start | bytes 344072 | tf_op jit(solution)/shard_map/ppermute | solution.py:467
  7.9 6.4 %collective-permute-start.1 = (f32[7,4,8,128]{3,2,1,0:T(8,128)}, f32[7,4,8,128]{3,2,1,0:T(8,128)S(1)}, u32[]{:S(2)}, u32[]{:S(2)}) collective-permute-start(f32[7,4,8,128]{3,2,1,0:T(8,128)} %get-tuple-element.24), channel_id=1, source_target_pairs={{0,31},{1,0},{2,1},{3,2},{4,3},{5,4},{6,5},{7,6},{8,7},{9,8},{10,9... | collective-permute-start | bytes 344072 | tf_op jit(solution)/shard_map/ppermute | solution.py:467
  8.5 35.8 %collective-permute-start.4 = (f32[4,64,128]{2,1,0:T(8,128)}, f32[4,64,128]{2,1,0:T(8,128)S(1)}, u32[]{:S(2)}, u32[]{:S(2)}) collective-permute-start(f32[4,64,128]{2,1,0:T(8,128)} %get-tuple-element.32), channel_id=1, source_target_pairs={{0,32},{32,64},{64,96},{96,128},{128,160},{160,192},{192,224},{224... | collective-permute-start | bytes 393224 | tf_op jit(solution)/shard_map/ppermute | solution.py:467
  10.5 33.8 %collective-permute-start.5 = (f32[4,64,128]{2,1,0:T(8,128)}, f32[4,64,128]{2,1,0:T(8,128)S(1)}, u32[]{:S(2)}, u32[]{:S(2)}) collective-permute-start(f32[4,64,128]{2,1,0:T(8,128)} %get-tuple-element.33), channel_id=1, source_target_pairs={{0,224},{32,0},{64,32},{96,64},{128,96},{160,128},{192,160},{224,1... | collective-permute-start | bytes 393224 | tf_op jit(solution)/shard_map/ppermute | solution.py:467
  14.3 0.6 copy-start.9
  14.3 0.7 copy-start.10
  20.5 18.4 %collective-permute-start.2 = (f32[608,128]{1,0:T(8,128)}, f32[608,128]{1,0:T(8,128)S(1)}, u32[]{:S(2)}, u32[]{:S(2)}) collective-permute-start(f32[608,128]{1,0:T(8,128)} %get-tuple-element.28), channel_id=1, source_target_pairs={{0,32},{32,64},{64,96},{96,128},{128,160},{160,192},{192,224},{224... | collective-permute-start | bytes 933896 | tf_op jit(solution)/shard_map/ppermute | solution.py:467
  21.2 17.7 %collective-permute-start.3 = (f32[608,128]{1,0:T(8,128)}, f32[608,128]{1,0:T(8,128)S(1)}, u32[]{:S(2)}, u32[]{:S(2)}) collective-permute-start(f32[608,128]{1,0:T(8,128)} %get-tuple-element.29), channel_id=1, source_target_pairs={{0,224},{32,0},{64,32},{96,64},{128,96},{160,128},{192,160},{224,1... | collective-permute-start | bytes 933896 | tf_op jit(solution)/shard_map/ppermute | solution.py:467
  35.4 26.0 %all-to-all-start = ((f32[8,16,8,128]{3,2,1,0:T(8,128)}), f32[8,16,8,128]{3,2,1,0:T(8,128)S(1)}, u32[]{:S(2)}, u32[]{:S(2)}) async-start(f32[8,16,8,128]{3,2,1,0:T(8,128)} %copy_bitcast_fusion), calls=%async_computation | async-start | bytes 1048576 | tf_op jit(solution)/shard_map/turn/all_to_all | solution.py:540
  38.9 5.4 %copy-start.3 = (f32[608,128]{1,0:T(8,128)}, f32[608,128]{1,0:T(8,128)S(1)}, u32[]{:S(2)}) copy-start(f32[608,128]{1,0:T(8,128)S(1)} %collective-permute-done.2.left_ref) | copy-start | bytes 933892
  38.9 5.4 %copy-start.4 = (f32[608,128]{1,0:T(8,128)}, f32[608,128]{1,0:T(8,128)S(1)}, u32[]{:S(2)}) copy-start(f32[608,128]{1,0:T(8,128)S(1)} %collective-permute-done.3.right_ref) | copy-start | bytes 933892
  38.9 22.5 %collective-permute-start.6 = (f32[576,128]{1,0:T(8,128)}, f32[576,128]{1,0:T(8,128)S(1)}, u32[]{:S(2)}, u32[]{:S(2)}) collective-permute-start(f32[576,128]{1,0:T(8,128)} %get-tuple-element.34), channel_id=1, source_target_pairs={{0,32},{32,64},{64,96},{96,128},{128,160},{160,192},{192,224},{224... | collective-permute-start | bytes 884744 | tf_op jit(solution)/shard_map/ppermute | solution.py:467
  41.9 20.0 %collective-permute-start.7 = (f32[576,128]{1,0:T(8,128)}, f32[576,128]{1,0:T(8,128)S(1)}, u32[]{:S(2)}, u32[]{:S(2)}) collective-permute-start(f32[576,128]{1,0:T(8,128)} %get-tuple-element.35), channel_id=1, source_target_pairs={{0,224},{32,0},{64,32},{96,64},{128,96},{160,128},{192,160},{224,1... | collective-permute-start | bytes 884744 | tf_op jit(solution)/shard_map/ppermute | solution.py:467
  44.3 0.7 copy-start.7
  44.9 0.7 copy-start.8
  61.4 0.8 copy-start.1
  61.4 0.9 copy-start.5
  61.8 0.7 copy-start.6

commit v3 on v2

--- a/solution.py
+++ b/solution.py
@@ -8,6 +8,7 @@
 from jax.sharding import Mesh
 from jax.sharding import PartitionSpec as P
 
+
 STEPS = 8
 ROW = ("row_0", "row_1")
 COL = ("col_0", "col_1", "col_2")
@@ -38,18 +39,12 @@
     return pltpu.roll(block, 64, 1)
 
 
-def prepare(e_hbm, h_hbm, c_hbm, t_hbm, up_ref, down_ref, cup_ref, cdown_ref, src, t_ref, sems):
-    comes = []
+def prepare(e_ref, h_ref, c_ref, t_ref, up_ref, down_ref, cup_ref, cdown_ref):
     for comp in range(7):
-        ref, at = ((e_hbm, comp) if comp < 3 else (h_hbm, comp - 3)) if comp < 6 else (c_hbm, 0)
-        comes.append(pltpu.make_async_copy(ref.at[at], src.at[comp], sems.at[comp]))
-        comes[comp].start()
-    goes = []
-    for comp in range(7):
-        comes[comp].wait()
+        src, at = ((e_ref, comp) if comp < 3 else (h_ref, comp - 3)) if comp < 6 else (c_ref, 0)
         for j in range(4):
             block = jnp.concatenate(
-                [src[comp, pl.ds(j, NZ, stride=8), :], src[comp, pl.ds(j + 4, NZ, stride=8), :]], 0
+                [src[at, pl.ds(j, NZ, stride=8), :], src[at, pl.ds(j + 4, NZ, stride=8), :]], 0
             )
             turned = block.T
             up_ref[comp, j] = turned[120:128]
@@ -68,28 +63,22 @@
             t_ref[comp, j + 4, 0:8] = before
             t_ref[comp, j, 72:80] = after
             t_ref[comp, j + 4, 72:80] = swap(after)
-        goes.append(pltpu.make_async_copy(t_ref.at[comp], t_hbm.at[comp], sems.at[7 + comp]))
-        goes[comp].start()
-    for go in goes:
-        go.wait()
-
-
-def fill(f, coef, t_hbm, below_hbm, above_hbm, halo, sems, first):
-    copies = []
-    for comp in range(6):
-        into = f.at[comp, pl.ds(first, 8), pl.ds(8, ROWS), :]
-        copies.append(pltpu.make_async_copy(t_hbm.at[comp], into, sems.at[comp]))
-    copies.append(pltpu.make_async_copy(t_hbm.at[6], coef.at[pl.ds(first, 8)], sems.at[6]))
-    copies.append(pltpu.make_async_copy(below_hbm, halo.at[0], sems.at[7]))
-    copies.append(pltpu.make_async_copy(above_hbm, halo.at[1], sems.at[8]))
-    return copies
-
-
-def merge(f, coef, halo, first, col, last):
+
+
+def fill(f, coef, t_ref, first):
+    for x in range(8):
+        for t in range(TILES):
+            rows = slice(8 * t, 8 * t + 8)
+            for comp in range(6):
+                f[comp, first + x, tile(t)] = t_ref[comp, x, rows]
+            coef[first + x, rows] = t_ref[6, x, rows]
+
+
+def merge(f, coef, below_ref, above_ref, first, col, last):
     low = lanes() < 64
     for comp in range(7):
         for x in range(8):
-            below, above = halo[0, comp, x % 4], halo[1, comp, x % 4]
+            below, above = below_ref[comp, x % 4], above_ref[comp, x % 4]
             below = jnp.where(col > 0, swap(below) if x >= 4 else below, 0.0)
             above = jnp.where(col < last, swap(above) if x < 4 else above, 0.0)
             if comp < 6:
@@ -112,7 +101,7 @@
 
 def tables(sc_ref, xt_ref, yt_ref, hc_ref, planes, full_x, full_y):
     widths = [sc_ref[i].astype(jnp.float32) for i in range(4)]
-    row, col = sc_ref[4], sc_ref[5]
+    row, col = lax.axis_index(ROW), lax.axis_index(COL)
     for p, x in planes:
         at = jnp.full((8, 128), (row * 8 + x).astype(jnp.float32))
         for k, shift in ((0, 0.5), (2, 0.0)):
@@ -228,20 +217,22 @@
             pl.when(i < number)(functools.partial(body, i))
 
 
-def alone(full_x, full_y, last, begin, end, sc, t_hbm, below_hbm, above_hbm, *rest):
-    up_ref, down_ref, f, psi, coef, xt, yt, hc, halo, sems = rest
-    col = sc[5]
-    copies = fill(f, coef, t_hbm, below_hbm, above_hbm, halo, sems, 1)
-    for copy in copies:
-        copy.start()
+def alone(full_x, full_y, last, begin, end, sc, t_ref, below_ref, above_ref, *rest):
+    col = lax.axis_index(COL)
+    if begin > 0:
+        (keep_ref, up_ref, down_ref), scratches = rest[:3], rest[3:]
+        for comp in range(7):
+            keep_ref[comp] = t_ref[comp]
+    else:
+        (up_ref, down_ref), scratches = rest[:2], rest[2:]
+    f, psi, coef, xt, yt, hc = scratches
+    fill(f, coef, t_ref, 1)
     tables(sc, xt, yt, hc, [(1 + x, x) for x in range(8)], full_x, full_y)
     zero_planes(psi, range(8), (1, 9), ROWS)
     zero_planes(f, range(6), (0, 1), ROWS + 16)
     zero_planes(f, range(6), (9, 10), ROWS + 16)
     zero_edges(f, 1)
-    for copy in copies:
-        copy.wait()
-    merge(f, coef, halo, 1, col, last)
+    merge(f, coef, below_ref, above_ref, 1, col, last)
     if begin == 0:
         low = lanes() < 64
         for k in range(DEEP):
@@ -332,21 +323,18 @@
 
 
 def joined(
-    full_x, full_y, last_row, last, early, sc, t_hbm, below_hbm, above_hbm, left_ref, right_ref, cleft_ref,
-    cright_ref, end_hbm, f, psi, coef, xt, yt, hc, halo, sems,
+    full_x, full_y, last_row, last, early, sc, t_ref, below_ref, above_ref, left_ref, right_ref, cleft_ref,
+    cright_ref, end_ref, f, psi, xt, yt, hc,
 ):
-    row, col = sc[4], sc[5]
-    copies = fill(f, coef, t_hbm, below_hbm, above_hbm, halo, sems, 6)
-    for copy in copies:
-        copy.start()
+    row, col = lax.axis_index(ROW), lax.axis_index(COL)
+    coef = end_ref.at[pl.ds(48, 20)]
+    fill(f, coef, t_ref, 6)
     tables(sc, xt, yt, hc, CELLS, full_x, full_y)
     zero_planes(psi, range(8), (1, 19), ROWS)
     zero_planes(f, range(6), (0, 6), ROWS + 16)
     zero_planes(f, range(6), (14, 20), ROWS + 16)
     zero_edges(f, 6)
-    for copy in copies:
-        copy.wait()
-    merge(f, coef, halo, 6, col, last)
+    merge(f, coef, below_ref, above_ref, 6, col, last)
     low = lanes() < 64
     for ref, edge_ref, first, there in (
         (cleft_ref, left_ref, 1, row > 0),
@@ -364,9 +352,6 @@
                     value = ref[k, 8 * t - 8 : 8 * t]
                 coef[first + k, 8 * t : 8 * t + 8] = jnp.where(there, value, 0.0)
 
-    out = pltpu.make_async_copy(coef, end_hbm.at[pl.ds(48, 20)], sems.at[6])
-    out.start()
-
     def step(s, carry):
         deep = jnp.minimum(s + 1, STEPS - s)
         at = 2 * jnp.minimum(s, early - 1)
@@ -381,30 +366,20 @@
         return carry
 
     lax.fori_loop(0, STEPS, step, 0)
-    out.wait()
-    outs = []
     for comp in range(6):
-        own = f.at[comp, pl.ds(6, 8), pl.ds(8, ROWS), :]
-        outs.append(pltpu.make_async_copy(own, end_hbm.at[pl.ds(8 * comp, 8)], sems.at[comp]))
-        outs[comp].start()
-    for copy in outs:
-        copy.wait()
+        for x in range(8):
+            end_ref[8 * comp + x, STEPS : STEPS + HALF] = f[comp, 6 + x, 8 + STEPS : 8 + STEPS + HALF]
 
 
 def late(
-    full_x, full_y, last_row, early, count, sc, snap, end_hbm, left_ref, right_ref, modes_hbm,
-    out_ref, e_out, h_out, f, psi, coef, xt, yt, hc, end_ref, modes_ref, planes, snaps, gram_ref, sems,
+    full_x, full_y, last_row, early, count, sc, snap, end_ref, left_ref, right_ref, modes_ref,
+    out_ref, e_out, h_out, f, psi, xt, yt, hc, planes, snaps, gram_ref, sems,
 ):
-    row = sc[4]
-    coef_in = pltpu.make_async_copy(end_hbm.at[pl.ds(48, 20)], coef, sems.at[2])
-    end_in = pltpu.make_async_copy(end_hbm.at[pl.ds(0, 48)], end_ref, sems.at[3])
-    modes_in = pltpu.make_async_copy(modes_hbm, modes_ref, sems.at[4])
-    for copy in (coef_in, end_in, modes_in):
-        copy.start()
+    row = lax.axis_index(ROW)
+    coef = end_ref.at[pl.ds(48, 20)]
     tables(sc, xt, yt, hc, CELLS, full_x, full_y)
     zero_planes(f, range(6), (2, 18), ROWS + 16)
     zero_planes(psi, range(8), (3, 17), ROWS)
-    coef_in.wait()
     count_late = STEPS - early
 
     def step(j, carry):
@@ -419,7 +394,6 @@
         return carry
 
     lax.fori_loop(0, count_late, step, 0)
-    end_in.wait()
 
     low = lax.broadcasted_iota(jnp.int32, (HALF, 128), 1) < 64
     own = slice(8 + STEPS, 8 + STEPS + HALF)
@@ -439,7 +413,6 @@
     ]
     for copy in copies:
         copy.start()
-    modes_in.wait()
     for s in range(count):
         snaps[8 * s : 8 * s + 8] = planes[pl.ds(pl.multiple_of(snap[s] * 8, 8), 8), :]
     gram = jnp.zeros((count, count), jnp.float32)
@@ -462,6 +435,14 @@
         copy.wait()
 
 
+def part_out(whole_ref, coef_ref, gram_ref):
+    for b in range(8):
+        coef_ref[8 * b : 8 * b + 8] = whole_ref[b, 0:8]
+        packed = whole_ref[b, 8:12]
+        gram_ref[4 * b : 4 * b + 4] = packed[:, :64]
+        gram_ref[32 + 4 * b : 36 + 4 * b] = packed[:, 64:]
+
+
 def around(block, axis, distance):
     size = lax.axis_size(axis)
     return lax.ppermute(block, axis, [(i, (i + distance) % size) for i in range(size)])
@@ -485,22 +466,19 @@
     )
 
 
-def scratch(planes, *more):
-    shapes = [(6, planes, ROWS + 16, 128), (8, planes, ROWS, 128), (planes, ROWS, 128)]
-    shapes = shapes + [(4, planes, 8, 128), (4, ROWS, 128), (2, ROWS, 128)] + list(more)
+def scratch(planes, coef):
+    shapes = [(6, planes, ROWS + 16, 128), (8, planes, ROWS, 128)] + [(planes, ROWS, 128)] * coef
+    shapes = shapes + [(4, planes, 8, 128), (4, ROWS, 128), (2, ROWS, 128)]
     return [pltpu.VMEM(shape, jnp.float32) for shape in shapes]
 
 
-HALO = (2, 7, 4, 8, 128)
 EARLY = 4
 
 
 def shards(e_field, h_field, e_coef, basis, pml_width, snap_index):
     rows_count, cols_count = lax.axis_size(ROW), lax.axis_size(COL)
     full_x, full_y = 8 * rows_count, 128 * cols_count
-    row, col = lax.axis_index(ROW), lax.axis_index(COL)
     count = snap_index.shape[0]
-    scalars = jnp.concatenate([pml_width, jnp.stack([row, col]).astype(jnp.int32)])
     vmem = pl.BlockSpec(memory_space=pltpu.VMEM)
     smem = pl.BlockSpec(memory_space=pltpu.SMEM)
     hbm = pl.BlockSpec(memory_space=pltpu.HBM)
@@ -508,77 +486,73 @@
     turned, up, down, c_up, c_down = call(
         prepare, 10**9, PREPARE_MIB,
         out_shape=(f32(7, 8, ROWS, 128),) + (f32(7, 4, 8, 128),) * 2 + (f32(4, HALF, 128),) * 2,
-        in_specs=[hbm] * 3,
-        out_specs=(hbm,) + (vmem,) * 4,
-        scratch_shapes=[
-            pltpu.VMEM((7, 512, 128), jnp.float32),
-            pltpu.VMEM((7, 8, ROWS, 128), jnp.float32),
-            pltpu.SemaphoreType.DMA((14,)),
-        ],
+        in_specs=[vmem] * 3,
+        out_specs=(vmem,) * 5,
     )(e_field.reshape(3, 512, 128), h_field.reshape(3, 512, 128), e_coef.reshape(1, 512, 128))
     below, above = around(up, COL, 1), around(down, COL, -1)
     c_left, c_right = around(c_up, ROW, 1), around(c_down, ROW, -1)
 
-    def run_alone(begin, end):
+    def run_alone(begin, end, turned, below, above):
         sent = f32(2 * (end - begin) * SENT + (8 * DEEP if begin == 0 else 0), 128)
         return call(
             functools.partial(alone, full_x, full_y, cols_count - 1, begin, end), 4 * 10**9, ALONE_MIB,
-            out_shape=(sent, sent),
-            in_specs=[smem] + [hbm] * 3,
-            out_specs=(vmem,) * 2,
-            scratch_shapes=scratch(10, HALO) + [pltpu.SemaphoreType.DMA((9,))],
-        )(scalars, turned, below, above)
-
-    with jax.named_scope("alone_a"):
-        up, down = run_alone(0, EARLY)
+            out_shape=((f32(7, 8, ROWS, 128),) if begin > 0 else ()) + (sent, sent),
+            in_specs=[smem] + [vmem] * 3,
+            out_specs=(vmem,) * (3 if begin > 0 else 2),
+            scratch_shapes=scratch(10, 1),
+        )(pml_width, turned, below, above)
+
+    up, down = run_alone(0, EARLY, turned, below, above)
+    up, down, *own = lax.optimization_barrier((up, down, turned, below, above))
     left, right = around(up, ROW, 1), around(down, ROW, -1)
-    with jax.named_scope("alone_b"):
-        up, down = run_alone(EARLY, STEPS)
-    with jax.named_scope("turn"):
-        modes, up = lax.optimization_barrier((basis, up))
-        modes = modes.reshape(16, rows_count, 8, 128).transpose(1, 0, 2, 3)
-        modes = lax.all_to_all(modes, ROW, split_axis=0, concat_axis=0, tiled=True).reshape(1024, 128)
+    turned_far, up, down = run_alone(EARLY, STEPS, *own)
+    modes, up = lax.optimization_barrier((basis, up))
+    modes = modes.reshape(16, rows_count, 8, 128).transpose(1, 0, 2, 3)
+    modes = lax.all_to_all(modes, ROW, split_axis=0, concat_axis=0, tiled=True).reshape(1024, 128)
     up, down, left, right = lax.optimization_barrier((up, down, left, right))
     left_late, right_late = around(up, ROW, 1), around(down, ROW, -1)
 
-    with jax.named_scope("joined"):
-        ends = call(
-            functools.partial(joined, full_x, full_y, rows_count - 1, cols_count - 1, EARLY), 12 * 10**9, JOINED_MIB,
-            out_shape=f32(68, ROWS, 128),
-            in_specs=[smem] + [hbm] * 3 + [vmem] * 4,
-            out_specs=hbm,
-            scratch_shapes=scratch(20, HALO) + [pltpu.SemaphoreType.DMA((9,))],
-        )(scalars, turned, below, above, left, right, c_left, c_right)
+    ends = call(
+        functools.partial(joined, full_x, full_y, rows_count - 1, cols_count - 1, EARLY), 12 * 10**9, JOINED_MIB,
+        out_shape=f32(68, ROWS, 128),
+        in_specs=[smem] + [vmem] * 7,
+        out_specs=vmem,
+        scratch_shapes=scratch(20, 0),
+    )(pml_width, turned_far, below, above, left, right, c_left, c_right)
 
     sums, e_final, h_final = call(
         functools.partial(late, full_x, full_y, rows_count - 1, EARLY, count), 4 * 10**9, LATE_MIB,
         out_shape=(f32(8, 12, 128), f32(1536, 128), f32(1536, 128)),
-        in_specs=[smem] * 2 + [hbm] + [vmem] * 2 + [hbm],
+        in_specs=[smem] * 2 + [vmem] * 4,
         out_specs=(vmem, hbm, hbm),
-        scratch_shapes=scratch(20, (48, ROWS, 128), (1024, 128))
+        scratch_shapes=scratch(20, 0)
         + [
             pltpu.VMEM((6 * NZ * 8, 128), jnp.float32),
             pltpu.VMEM((count * 8, 128), jnp.float32),
             pltpu.VMEM((32, 128), jnp.float32),
-            pltpu.SemaphoreType.DMA((5,)),
+            pltpu.SemaphoreType.DMA((2,)),
         ],
-    )(scalars, snap_index, ends, left_late, right_late, modes)
+    )(pml_width, snap_index, ends, left_late, right_late, modes)
 
     part = lax.all_to_all(sums, NEAR, split_axis=0, concat_axis=0, tiled=True).sum(0)
     part = spread(part, FAR, lax.axis_size(FAR)).sum(0)
     whole = spread(part, NEAR, lax.axis_size(NEAR))
-    coefficients = whole[:, :8].reshape(count, 128)
-    packed = whole[:, 8:].reshape(count // 2, 128)
-    gram = jnp.concatenate([packed[:, :64], packed[:, 64:]], 0)
+    coefficients, gram = call(
+        part_out, 10**6, 4,
+        out_shape=(f32(count, 128), f32(count, count)),
+        in_specs=[vmem],
+        out_specs=(vmem,) * 2,
+    )(whole)
     shape = e_field.shape
     return (e_final.reshape(shape), h_final.reshape(shape), coefficients, gram)
 
 
-PREPARE_MIB, ALONE_MIB, JOINED_MIB, LATE_MIB = 56, 60, 60, 60
+PREPARE_MIB, ALONE_MIB, JOINED_MIB, LATE_MIB = 12, 14, 24, 28
 
 
 def solution(mesh):
     split = Mesh(mesh.devices.reshape(4, 2, 8, 2, 2), ROW + COL)
+
     return jax.shard_map(
         shards,
         mesh=split,

time: 118 us -> 112 us (0.949)
  Pallas kernels: 44.7 us -> 34 us
  local copies, waits for them, and re-layouts: 4.25 us -> 11.4 us
  other arithmetic: 1.34 us -> 0.05 us
    unnamed x22 -> x24, local copies, waits for them, and re-layouts: 2.7 us -> 10.6 us
    pallas_call x2, Pallas kernels: 14.4 us -> 10 us  [run_alone(): call(functools.partial(alone, full_x, full_y, cols_count - 1, begin, end)...]
    pallas_call x1, Pallas kernels: 4.47 us -> 1.07 us  [shards(): call(prepare, 10 ** 9, PREPARE_MIB, out_shape=(f32(7, 8, ROWS, 128),) + (...]
    pallas_call x1, Pallas kernels: 15.8 us -> 13.6 us  [shards(): call(functools.partial(joined, full_x, full_y, rows_count - 1, cols_count...]
    pallas_call x1, Pallas kernels: 10 us -> 8.67 us  [shards(): call(functools.partial(late, full_x, full_y, rows_count - 1, EARLY, count...]
    concatenate x2 -> x0, other arithmetic: 1.29 us -> none  [the longest x1 0.67 us: shards(): jnp.concatenate([pml_width, jnp.stack([row, col]).astype(jnp.int32)])]
  transfers between devices with their start and end apart: 9 -> 9, of which waited for: 1 -> 0; matrix products, arithmetic and copies ran while one was open for 1% -> 1% of each run, Pallas kernels for 26% -> 21%
where the time goes in v3:
time: 112 us; the launch traced here: 111 us
  blocking collectives  42.7 us (38%)
  Pallas kernels  34 us (30%)
  starting transfers between devices  22.4 us (20%)
  local copies, waits for them, and re-layouts  11.4 us (10%)
    all_to_all x2, blocking collectives, spread(): return lax.all_to_all(whole, axes, split_axis=0, concat_axis=0, tiled=True)  29.2 us
    ppermute x8, starting transfers between devices, around(): lax.ppermute(block, axis, [(i, (i + distance) % size) for i in range(size)])  19 us
    pallas_call x1, Pallas kernels, shards(): call(functools.partial(joined, full_x, full_y, rows_count - 1, cols_count...  13.6 us
    all_to_all x1, blocking collectives, shards(): lax.all_to_all(sums, NEAR, split_axis=0, concat_axis=0, tiled=True).sum(0)  13.5 us
    unnamed x24, local copies, waits for them, and re-layouts  10.6 us
    pallas_call x2, Pallas kernels, run_alone(): call(functools.partial(alone, full_x, full_y, cols_count - 1, begin, end)...  10 us
    pallas_call x1, Pallas kernels, shards(): call(functools.partial(late, full_x, full_y, rows_count - 1, EARLY, count...  8.67 us
    all_to_all x1, starting transfers between devices, shards(): lax.all_to_all(modes, ROW, split_axis=0, concat_axis=0, tiled=True)  3.49 us
  transfers between devices with their start and end apart: 9, of which 0 were waited for; matrix products, arithmetic and copies ran while one was open for 1% of the time, Pallas kernels for 21%

profile of v3, /device:TPU:1, one launch (start us, length us, event | category | flops | bytes accessed | tf_op | source)
XLA Modules:
  0.0 111.4 jit_solution(14802800345458060884)
XLA Ops:
  0.6 0.0 copy-start
  0.7 1.2 %copy-done.1 = f32[3,64,8,128]{3,2,1,0:T(8,128)S(1)} copy-done((f32[3,64,8,128]{3,2,1,0:T(8,128)S(1)}, f32[3,64,8,128]{3,2,1,0:T(8,128)}, u32[]{:S(2)}) %copy-start.1) | copy-done | bytes 786456
  1.9 1.1 %copy-done.2 = f32[3,64,8,128]{3,2,1,0:T(8,128)S(1)} copy-done((f32[3,64,8,128]{3,2,1,0:T(8,128)S(1)}, f32[3,64,8,128]{3,2,1,0:T(8,128)}, u32[]{:S(2)}) %copy-start.2) | copy-done | bytes 786456
  3.0 0.9 copy-done.3
  3.9 1.1 shard_map.93
  5.0 2.8 %collective-permute-start = (f32[7,4,8,128]{3,2,1,0:T(8,128)S(1)}, f32[7,4,8,128]{3,2,1,0:T(8,128)S(1)}, u32[]{:S(2)}, u32[]{:S(2)}) collective-permute-start(f32[7,4,8,128]{3,2,1,0:T(8,128)S(1)} %get-tuple-element.31), channel_id=1, source_target_pairs={{0,1},{1,2},{2,3},{3,4},{4,5},{5,6},{6,7},{7,8},{8,9},{9,10},{10,1... | collective-permute-start | bytes 344072 | tf_op jit(solution)/shard_map/ppermute | solution.py:448
  7.8 0.6 collective-permute-start.1
  8.4 2.0 %collective-permute-start.4 = (f32[4,64,128]{2,1,0:T(8,128)S(1)}, f32[4,64,128]{2,1,0:T(8,128)S(1)}, u32[]{:S(2)}, u32[]{:S(2)}) collective-permute-start(f32[4,64,128]{2,1,0:T(8,128)S(1)} %get-tuple-element.46), channel_id=1, source_target_pairs={{0,32},{32,64},{64,96},{96,128},{128,160},{160,192},{192,224},{224... | collective-permute-start | bytes 393224 | tf_op jit(solution)/shard_map/ppermute | solution.py:448
  10.4 3.1 %collective-permute-start.5 = (f32[4,64,128]{2,1,0:T(8,128)S(1)}, f32[4,64,128]{2,1,0:T(8,128)S(1)}, u32[]{:S(2)}, u32[]{:S(2)}) collective-permute-start(f32[4,64,128]{2,1,0:T(8,128)S(1)} %get-tuple-element.47), channel_id=1, source_target_pairs={{0,224},{32,0},{64,32},{96,64},{128,96},{160,128},{192,160},{224,1... | collective-permute-start | bytes 393224 | tf_op jit(solution)/shard_map/ppermute | solution.py:448
  13.5 0.0 collective-permute-done.below_ref
  13.5 0.0 collective-permute-done.1.above_ref
  13.5 3.3 %shard_map.94 = (f32[608,128]{1,0:T(8,128)S(1)}, f32[608,128]{1,0:T(8,128)S(1)}) custom-call(s32[4]{0:T(128)S(1)} %copy-done.6, f32[7,8,80,128]{3,2,1,0:T(8,128)S(1)} %get-tuple-element.35.t_ref, f32[7,4,8,128]{3,2,1,0:T(8,128)S(1)} %collective-permute-done.below_ref, f32[7,4,8,128]{3,2,1,0:T(8,128)S(1)} %collective-permute-done.1.above_ref), custom_call_target="tpu_custom_call" | custom-call | flops 4000000000 | bytes 4000000 | tf_op jit(solution)/shard_map/pallas_call | solution.py:497
  16.8 1.2 %collective-permute-start.2 = (f32[608,128]{1,0:T(8,128)S(1)}, f32[608,128]{1,0:T(8,128)S(1)}, u32[]{:S(2)}, u32[]{:S(2)}) collective-permute-start(f32[608,128]{1,0:T(8,128)S(1)} %get-tuple-element.42), channel_id=1, source_target_pairs={{0,32},{32,64},{64,96},{96,128},{128,160},{160,192},{192,224},{224... | collective-permute-start | bytes 933896 | tf_op jit(solution)/shard_map/ppermute | solution.py:448
  18.0 4.0 %collective-permute-start.3 = (f32[608,128]{1,0:T(8,128)S(1)}, f32[608,128]{1,0:T(8,128)S(1)}, u32[]{:S(2)}, u32[]{:S(2)}) collective-permute-start(f32[608,128]{1,0:T(8,128)S(1)} %get-tuple-element.43), channel_id=1, source_target_pairs={{0,224},{32,0},{64,32},{96,64},{128,96},{160,128},{192,160},{224,1... | collective-permute-start | bytes 933896 | tf_op jit(solution)/shard_map/ppermute | solution.py:448
  21.9 6.8 %shard_map.95 = (f32[7,8,80,128]{3,2,1,0:T(8,128)S(1)}, f32[576,128]{1,0:T(8,128)S(1)}, f32[576,128]{1,0:T(8,128)S(1)}) custom-call(s32[4]{0:T(128)S(1)} %copy-done.6, f32[7,8,80,128]{3,2,1,0:T(8,128)S(1)} %get-tuple-element.35.t_ref, f32[7,4,8,128]{3,2,1,0:T(8,128)S(1)} %collective-permute-done.below_ref, f32[7,4,8,128]{3,2,1,0:T(8,128)S(1)} %collective-permute-done.1.above_ref), custom_call_target="tpu_custom_call" | custom-call | flops 4000000000 | bytes 4000000 | tf_op jit(solution)/shard_map/pallas_call | solution.py:497
  28.7 1.4 %copy-done.10 = f32[7,8,80,128]{3,2,1,0:T(8,128)} copy-done((f32[7,8,80,128]{3,2,1,0:T(8,128)}, f32[7,8,80,128]{3,2,1,0:T(8,128)S(1)}, u32[]{:S(2)}) %copy-start.10) | copy-done | bytes 2293784
  30.1 0.8 copy_bitcast_fusion
  30.9 3.5 %all-to-all-start = ((f32[8,16,8,128]{3,2,1,0:T(8,128)}), f32[8,16,8,128]{3,2,1,0:T(8,128)S(1)}, u32[]{:S(2)}, u32[]{:S(2)}) async-start(f32[8,16,8,128]{3,2,1,0:T(8,128)} %copy_bitcast_fusion), calls=%async_computation | async-start | bytes 1048576 | tf_op jit(solution)/shard_map/all_to_all | solution.py:511
  34.5 0.0 collective-permute-done.2.left_ref
  34.5 2.9 %collective-permute-start.6 = (f32[576,128]{1,0:T(8,128)S(1)}, f32[576,128]{1,0:T(8,128)S(1)}, u32[]{:S(2)}, u32[]{:S(2)}) collective-permute-start(f32[576,128]{1,0:T(8,128)S(1)} %get-tuple-element.48), channel_id=1, source_target_pairs={{0,32},{32,64},{64,96},{96,128},{128,160},{160,192},{192,224},{224... | collective-permute-start | bytes 884744 | tf_op jit(solution)/shard_map/ppermute | solution.py:448
  37.4 2.4 %collective-permute-start.7 = (f32[576,128]{1,0:T(8,128)S(1)}, f32[576,128]{1,0:T(8,128)S(1)}, u32[]{:S(2)}, u32[]{:S(2)}) collective-permute-start(f32[576,128]{1,0:T(8,128)S(1)} %get-tuple-element.49), channel_id=1, source_target_pairs={{0,224},{32,0},{64,32},{96,64},{128,96},{160,128},{192,160},{224,1... | collective-permute-start | bytes 884744 | tf_op jit(solution)/shard_map/ppermute | solution.py:448
  39.8 0.0 collective-permute-done.5.cright_ref
  39.8 0.9 copy-done.5
  40.7 1.6 %copy-done.11 = f32[7,8,80,128]{3,2,1,0:T(8,128)S(1)} copy-done((f32[7,8,80,128]{3,2,1,0:T(8,128)S(1)}, f32[7,8,80,128]{3,2,1,0:T(8,128)}, u32[]{:S(2)}) %copy-start.11) | copy-done | bytes 2293784
  42.4 13.6 %shard_map.96.end_ref = f32[68,80,128]{2,1,0:T(8,128)S(1)} custom-call(s32[4]{0:T(128)S(1)} %copy-done.6, f32[7,8,80,128]{3,2,1,0:T(8,128)S(1)} %copy-done.11, f32[7,4,8,128]{3,2,1,0:T(8,128)S(1)} %collective-permute-done.below_ref, f32[7,4,8,128]{3,2,1,0:T(8,128)S(1)} %copy-done.5, f32[608,128]{1,0:T(8,128)S(1)} %collective-permute-done.2.left_ref, ...), custom_call_target="tpu_custom_call" | custom-call | flops 12000000000 | bytes 4000000 | tf_op jit(solution)/shard_map/pallas_call | solution.py:515
  56.0 1.5 %copy-done.8 = f32[68,80,128]{2,1,0:T(8,128)} copy-done((f32[68,80,128]{2,1,0:T(8,128)}, f32[68,80,128]{2,1,0:T(8,128)S(1)}, u32[]{:S(2)}) %copy-start.8) | copy-done | bytes 2785304
  57.5 1.8 %copy-done.9 = f32[68,80,128]{2,1,0:T(8,128)S(1)} copy-done((f32[68,80,128]{2,1,0:T(8,128)S(1)}, f32[68,80,128]{2,1,0:T(8,128)}, u32[]{:S(2)}) %copy-start.9) | copy-done | bytes 2785304
  59.3 8.7 %shard_map.97 = (f32[8,12,128]{2,1,0:T(8,128)S(1)}, f32[1536,128]{1,0:T(8,128)}, f32[1536,128]{1,0:T(8,128)}) custom-call(s32[4]{0:T(128)S(1)} %copy-done.6, s32[64]{0:T(128)S(1)} %copy-done.7, f32[68,80,128]{2,1,0:T(8,128)S(1)} %copy-done.9, f32[576,128]{1,0:T(8,128)S(1)} %collective-permute-done.6.left_ref, ...), custom_call_target="tpu_custom_call" | custom-call | flops 4000000000 | bytes 4000000 | tf_op jit(solution)/shard_map/pallas_call | solution.py:523
  68.0 13.5 %all_to_all.20 = f32[8,12,128]{2,1,0:T(8,128)S(1)} all-to-all(f32[8,12,128]{2,1,0:T(8,128)S(1)} %get-tuple-element.53), channel_id=1, replica_groups=mesh['row_0'=4,'row_1'=2,'col_0'=8,'col_1'=2,'col_2'=2] {'row_1','col_1'..., dimensions={0} | all-to-all | bytes 98304 | tf_op jit(solution)/shard_map/all_to_all | solution.py:537
  81.5 18.2 %all_to_all.21 = f32[32,12,128]{2,1,0:T(8,128)S(1)} all-to-all(f32[32,12,128]{2,1,0:T(8,128)S(1)} %broadcast_in_dim.6), channel_id=1, replica_groups=mesh['row_0'=4,'row_1'=2,'col_0'=8,'col_1'=2,'col_2'=2] {'row_0','col_0'}, dimensions={0} | all-to-all | bytes 393216 | tf_op jit(solution)/shard_map/all_to_all | solution.py:453
  99.8 11.0 %all_to_all.22.whole_ref = f32[8,12,128]{2,1,0:T(8,128)S(1)} all-to-all(f32[8,12,128]{2,1,0:T(8,128)S(1)} %broadcast_in_dim.7), channel_id=1, replica_groups=mesh['row_0'=4,'row_1'=2,'col_0'=8,'col_1'=2,'col_2'=2] {'row_1','col_1'..., dimensions={0} | all-to-all | bytes 98304 | tf_op jit(solution)/shard_map/all_to_all | solution.py:453
  110.8 0.7 shard_map.98
  (24 shorter events, 0.1 us)
Async XLA Ops:
  0.6 29.5 %copy-start = (f32[16,64,128]{2,1,0:T(8,128)S(1)}, f32[16,64,128]{2,1,0:T(8,128)}, u32[]{:S(2)}) copy-start(f32[16,64,128]{2,1,0:T(8,128)} %param.9) | copy-start | bytes 1572868
  0.6 12.8 %copy-start.6 = (s32[4]{0:T(128)S(1)}, s32[4]{0:T(128)}, u32[]{:S(2)}) copy-start(s32[4]{0:T(128)} %sc.7) | copy-start | bytes 52
  0.7 1.2 %copy-start.1 = (f32[3,64,8,128]{3,2,1,0:T(8,128)S(1)}, f32[3,64,8,128]{3,2,1,0:T(8,128)}, u32[]{:S(2)}) copy-start(f32[3,64,8,128]{3,2,1,0:T(8,128)} %param.6) | copy-start | bytes 2359300
  1.9 1.1 %copy-start.2 = (f32[3,64,8,128]{3,2,1,0:T(8,128)S(1)}, f32[3,64,8,128]{3,2,1,0:T(8,128)}, u32[]{:S(2)}) copy-start(f32[3,64,8,128]{3,2,1,0:T(8,128)} %param.7) | copy-start | bytes 2359300
  3.0 0.9 copy-start.3
  5.0 8.5 %collective-permute-start = (f32[7,4,8,128]{3,2,1,0:T(8,128)S(1)}, f32[7,4,8,128]{3,2,1,0:T(8,128)S(1)}, u32[]{:S(2)}, u32[]{:S(2)}) collective-permute-start(f32[7,4,8,128]{3,2,1,0:T(8,128)S(1)} %get-tuple-element.31), channel_id=1, source_target_pairs={{0,1},{1,2},{2,3},{3,4},{4,5},{5,6},{6,7},{7,8},{8,9},{9,10},{10,1... | collective-permute-start | bytes 344072 | tf_op jit(solution)/shard_map/ppermute | solution.py:448
  7.8 5.7 %collective-permute-start.1 = (f32[7,4,8,128]{3,2,1,0:T(8,128)S(1)}, f32[7,4,8,128]{3,2,1,0:T(8,128)S(1)}, u32[]{:S(2)}, u32[]{:S(2)}) collective-permute-start(f32[7,4,8,128]{3,2,1,0:T(8,128)S(1)} %get-tuple-element.32), channel_id=1, source_target_pairs={{0,31},{1,0},{2,1},{3,2},{4,3},{5,4},{6,5},{7,6},{8,7},{9,8},{10,9... | collective-permute-start | bytes 344072 | tf_op jit(solution)/shard_map/ppermute | solution.py:448
  8.4 31.4 %collective-permute-start.4 = (f32[4,64,128]{2,1,0:T(8,128)S(1)}, f32[4,64,128]{2,1,0:T(8,128)S(1)}, u32[]{:S(2)}, u32[]{:S(2)}) collective-permute-start(f32[4,64,128]{2,1,0:T(8,128)S(1)} %get-tuple-element.46), channel_id=1, source_target_pairs={{0,32},{32,64},{64,96},{96,128},{128,160},{160,192},{192,224},{224... | collective-permute-start | bytes 393224 | tf_op jit(solution)/shard_map/ppermute | solution.py:448
  10.4 29.4 %collective-permute-start.5 = (f32[4,64,128]{2,1,0:T(8,128)S(1)}, f32[4,64,128]{2,1,0:T(8,128)S(1)}, u32[]{:S(2)}, u32[]{:S(2)}) collective-permute-start(f32[4,64,128]{2,1,0:T(8,128)S(1)} %get-tuple-element.47), channel_id=1, source_target_pairs={{0,224},{32,0},{64,32},{96,64},{128,96},{160,128},{192,160},{224,1... | collective-permute-start | bytes 393224 | tf_op jit(solution)/shard_map/ppermute | solution.py:448
  13.5 8.4 %copy-start.4 = (f32[7,4,8,128]{3,2,1,0:T(8,128)}, f32[7,4,8,128]{3,2,1,0:T(8,128)S(1)}, u32[]{:S(2)}) copy-start(f32[7,4,8,128]{3,2,1,0:T(8,128)S(1)} %collective-permute-done.1.above_ref) | copy-start | bytes 344068
  16.8 17.7 %collective-permute-start.2 = (f32[608,128]{1,0:T(8,128)S(1)}, f32[608,128]{1,0:T(8,128)S(1)}, u32[]{:S(2)}, u32[]{:S(2)}) collective-permute-start(f32[608,128]{1,0:T(8,128)S(1)} %get-tuple-element.42), channel_id=1, source_target_pairs={{0,32},{32,64},{64,96},{96,128},{128,160},{160,192},{192,224},{224... | collective-permute-start | bytes 933896 | tf_op jit(solution)/shard_map/ppermute | solution.py:448
  18.0 16.5 %collective-permute-start.3 = (f32[608,128]{1,0:T(8,128)S(1)}, f32[608,128]{1,0:T(8,128)S(1)}, u32[]{:S(2)}, u32[]{:S(2)}) collective-permute-start(f32[608,128]{1,0:T(8,128)S(1)} %get-tuple-element.43), channel_id=1, source_target_pairs={{0,224},{32,0},{64,32},{96,64},{128,96},{160,128},{192,160},{224,1... | collective-permute-start | bytes 933896 | tf_op jit(solution)/shard_map/ppermute | solution.py:448
  28.7 1.4 %copy-start.10 = (f32[7,8,80,128]{3,2,1,0:T(8,128)}, f32[7,8,80,128]{3,2,1,0:T(8,128)S(1)}, u32[]{:S(2)}) copy-start(f32[7,8,80,128]{3,2,1,0:T(8,128)S(1)} %get-tuple-element.38.t_ref) | copy-start | bytes 6881284
  30.9 26.6 %all-to-all-start = ((f32[8,16,8,128]{3,2,1,0:T(8,128)}), f32[8,16,8,128]{3,2,1,0:T(8,128)S(1)}, u32[]{:S(2)}, u32[]{:S(2)}) async-start(f32[8,16,8,128]{3,2,1,0:T(8,128)} %copy_bitcast_fusion), calls=%async_computation | async-start | bytes 1048576 | tf_op jit(solution)/shard_map/all_to_all | solution.py:511
  34.5 23.0 %collective-permute-start.6 = (f32[576,128]{1,0:T(8,128)S(1)}, f32[576,128]{1,0:T(8,128)S(1)}, u32[]{:S(2)}, u32[]{:S(2)}) collective-permute-start(f32[576,128]{1,0:T(8,128)S(1)} %get-tuple-element.48), channel_id=1, source_target_pairs={{0,32},{32,64},{64,96},{96,128},{128,160},{160,192},{192,224},{224... | collective-permute-start | bytes 884744 | tf_op jit(solution)/shard_map/ppermute | solution.py:448
  37.4 20.1 %collective-permute-start.7 = (f32[576,128]{1,0:T(8,128)S(1)}, f32[576,128]{1,0:T(8,128)S(1)}, u32[]{:S(2)}, u32[]{:S(2)}) collective-permute-start(f32[576,128]{1,0:T(8,128)S(1)} %get-tuple-element.49), channel_id=1, source_target_pairs={{0,224},{32,0},{64,32},{96,64},{128,96},{160,128},{192,160},{224,1... | collective-permute-start | bytes 884744 | tf_op jit(solution)/shard_map/ppermute | solution.py:448
  39.8 0.9 copy-start.5
  40.7 1.6 %copy-start.11 = (f32[7,8,80,128]{3,2,1,0:T(8,128)S(1)}, f32[7,8,80,128]{3,2,1,0:T(8,128)}, u32[]{:S(2)}) copy-start(f32[7,8,80,128]{3,2,1,0:T(8,128)} %copy-done.10) | copy-start | bytes 6881284
  42.4 15.1 %copy-start.7 = (s32[64]{0:T(128)S(1)}, s32[64]{0:T(128)}, u32[]{:S(2)}) copy-start(s32[64]{0:T(128)} %snap.1) | copy-start | bytes 772
  55.9 1.6 %copy-start.8 = (f32[68,80,128]{2,1,0:T(8,128)}, f32[68,80,128]{2,1,0:T(8,128)S(1)}, u32[]{:S(2)}) copy-start(f32[68,80,128]{2,1,0:T(8,128)S(1)} %shard_map.96.end_ref) | copy-start | bytes 8355844
  57.5 1.8 %copy-start.9 = (f32[68,80,128]{2,1,0:T(8,128)S(1)}, f32[68,80,128]{2,1,0:T(8,128)}, u32[]{:S(2)}) copy-start(f32[68,80,128]{2,1,0:T(8,128)} %copy-done.8) | copy-start | bytes 8355844
